TPU v7x, 128 devices: a whole 4x4x4 slice. The times are simulated.
128 devices in a mesh: member: 16 (over y_hi, z, core), dp: 8 (over x, y_lo).
Axes of the slice: x: 4, y: 4 (y_hi: 2, y_lo: 2; y = y_hi * 2 + y_lo), z: 4, core: 2. Of those that a mesh axis runs over, the one named last changes fastest.
Arguments:
- feats: bfloat16 [16, 4096, 1024], P('member', 'dp'), may hold values from -160 to 160
- pair_weight: float32 [16, 3], replicated, may hold values from 0.5 to 2
Outputs:
- grad_centred: float32 [16, 4096, 1024], P('member', 'dp')
- cka: float32 [16, 3], P('member')
All inputs are finite; a program needn't handle non-finite values.
Results may differ from a plain program's by a relative error of at most 0.0053.
Values may be sent and summed in bfloat16 or wider, within the bound.
No kernel may reach another device: no remote copies, remote signals or barrier semaphores. Data moves between devices by JAX's collectives and lax.ppermute only.
A program may use at most 128 MiB of HBM per device.

v0:
```python
import math

import jax
import jax.numpy as jnp
from jax import lax
from jax.sharding import Mesh
from jax.sharding import PartitionSpec as P

DP = ("dp_0", "dp_1")


def of_everyone(value, axis):
    copies = jnp.broadcast_to(value, (lax.axis_size(axis), *value.shape))
    return lax.all_to_all(copies, axis, split_axis=0, concat_axis=0, tiled=True)


def moved(value, axis, steps):
    count = lax.axis_size(axis)
    return lax.ppermute(value, axis, [(s, (s + steps) % count) for s in range(count)])


def moved_some(value, first, steps):
    count = lax.axis_size("member")
    return lax.ppermute(value, "member", [(s, (s + steps) % count) for s in range(first, count, 2)])


def swapped(value):
    return lax.ppermute(value, "member", [(s, s ^ 1) for s in range(lax.axis_size("member"))])


def crossing(value, from_even, from_odd):
    count = lax.axis_size("member")
    pairs = [(s, (s + (from_odd if s % 2 else from_even)) % count) for s in range(count)]
    return lax.ppermute(value, "member", pairs)


def after(value, *others):
    return lax.optimization_barrier((value, others))[0]


def wide_dot(a, b, left, right):
    return lax.dot_general(a, b, (((left,), (right,)), ((), ())), preferred_element_type=jnp.float32)


def f32(value):
    return value.astype(jnp.float32)


def bf16(value):
    return value.astype(jnp.bfloat16)


def body(feats, pair_weight):
    rows = feats[0]
    height, width = rows.shape
    around = lax.axis_size("dp_0")
    batch = height * lax.axis_size(DP)
    block = width // around
    half = width // 2
    x = lax.axis_index("dp_0")
    member = lax.axis_index("member")
    even = member % 2 == 0
    cut = (slice(0, half), slice(half, width))

    def columns(value, index):
        return lax.dynamic_slice_in_dim(value, index * block, block, axis=value.ndim - 1)

    mean = jnp.sum(of_everyone(jnp.sum(f32(rows), axis=0), DP), axis=0) / batch

    own = [columns(rows, x)]
    for d in range(1, around):
        own.append(moved(columns(rows, (x - d) % around), "dp_0", -d))
    block_mean = columns(mean, x)
    own = jnp.concatenate([bf16(f32(o) - block_mean) for o in own], axis=0)

    second = moved(own, "member", -2)
    crossed = swapped(second)
    step = moved(own, "member", 1)
    far = moved_some(step, 0, 2)
    third = jnp.where(even, far, step)
    blocks = [own, second, crossed, third]

    h0, h1 = rows[: height // 2], rows[height // 2 :]
    p0 = moved(h0, "dp_0", 1)
    m0 = moved(h0, "dp_0", -1)
    m1 = moved(h1, "dp_0", -1)
    p1 = moved(h1, "dp_0", 1)
    f0 = moved(p0, "dp_0", 1)
    f1 = moved(m1, "dp_0", -1)
    centred = jnp.concatenate([bf16(f32(v) - mean) for v in (h0, h1, m0, m1, f0, f1, p0, p1)], axis=0)

    def pair_sum(k):
        part = bf16(wide_dot(centred, blocks[k], 0, 0))
        return f32(part) + f32(moved(part, "dp_1", 1))

    covs = [pair_sum(k) for k in range(4)]

    def over_ring(value, first=(), second=()):
        for bit, others in ((1, first), (2, second)):
            come = lax.ppermute(value, "dp_0", [(s, s ^ bit) for s in range(around)])
            value = value + after(come, *others)
        return value

    def square_rows(ks):
        lines = jnp.arange(8)[:, None]
        return sum(jnp.where(lines == k, jnp.sum(covs[k] * covs[k], axis=0)[None], 0.0) for k in ks)

    def filled(lines):
        ones = jnp.ones((block, block), jnp.float32)
        return lax.dot_general(lines, ones, (((1,), (0,)), ((), ())), precision=lax.Precision.HIGHEST)

    members, pairs = pair_weight.shape

    def either(a, b):
        return jnp.where(even, a, b)

    wanted = (
        (member, 1),
        (member, either(2, 0)),
        (either(member - 3, member - 1), either(2, 0)),
        (member, 0),
        (member, 2),
        (member - 2, 1),
        (member - 1, 0),
        (member - 3, 2),
    )
    places = jnp.stack([(q % members) * pairs + column for q, column in wanted])
    picked = (jnp.arange(members * pairs)[None] == places[:, None]).astype(jnp.float32)
    weights = jnp.sum(picked * pair_weight.reshape(1, -1), axis=1, keepdims=True)
    weights = lax.optimization_barrier(jnp.broadcast_to(weights, (len(wanted), block)))
    weights = [weights[i : i + 1] for i in range(len(wanted))]

    hself = filled(over_ring(square_rows((0,))))
    h_p2 = moved(hself, "member", -2)
    h_s2 = crossing(hself, -1, -3)
    h_s3 = crossing(hself, 1, 3)
    hself, h_p2, h_s2, h_s3 = (v[:1] for v in (hself, h_p2, h_s2, h_s3))

    coefs = [2.0 * w / jnp.sqrt(hself * h) for w, h in zip(weights, (h_p2, h_s2, h_s3))]
    coefs = lax.optimization_barrier(coefs)
    mixer = {k: bf16(coefs[k - 1] * covs[k]) for k in (1, 2, 3)}
    mixers = jnp.concatenate([mixer[k] for k in (1, 2, 3)], axis=1)

    partners = jnp.concatenate(blocks[1:], axis=1)

    def share(d, h):
        return wide_dot(partners[d * height : (d + 1) * height], mixers[cut[h]], 1, 1)

    def own_share():
        return wide_dot(partners[:height], mixers, 1, 1)

    def outgoing(cov):
        return wide_dot(centred, cov, 1, 0)

    out3 = bf16(outgoing(mixer[3]))
    near = moved(out3, "member", -1)
    out2 = bf16(outgoing(mixer[2]))
    out2 = swapped(out2)
    back3 = jnp.where(even, near, moved_some(near, 1, -2))
    a0 = moved(bf16(share(2, 0)), "dp_0", 1)
    c0 = moved(bf16(share(3, 0)), "dp_0", -1)
    out1 = bf16(outgoing(mixer[1]) + f32(out2))
    back1 = moved(out1, "member", 2)
    a1 = moved(bf16(share(2, 1)), "dp_0", -1)
    c1_sent = bf16(share(1, 1))
    c1 = moved(c1_sent, "dp_0", 1)
    b0 = bf16(share(1, 0) + f32(a0))
    b0 = moved(b0, "dp_0", 1)
    self_term = bf16(outgoing(bf16(covs[0]))).reshape(around, height, block)
    self_parts = [self_term[0]] + [moved(self_term[d], "dp_0", d) for d in range(1, around)]
    b1_sent = bf16(share(3, 1) + f32(a1))
    b1 = moved(b1_sent, "dp_0", -1)
    sums = filled(over_ring(square_rows((1, 2, 3)), (c1_sent,), (b1_sent,)))
    sums, hself, h_p2, h_s2, h_s3 = lax.optimization_barrier((sums, hself, h_p2, h_s2, h_s3))
    cka2 = sums[1:2] / jnp.sqrt(hself * h_p2)
    held2 = sums[2:3] / jnp.sqrt(hself * h_s2)
    held3 = sums[3:4] / jnp.sqrt(h_s3 * hself)
    lines = jnp.arange(8)[:, None]
    ckas = jnp.where(lines == 1, cka2, jnp.where(lines == 2, held2, held3))
    own_part = weights[0] * cka2
    own_part = own_part + either(weights[4], weights[3]) * held2 + either(weights[7], weights[6]) * held3
    ckas, own_part, scale = lax.optimization_barrier((ckas, own_part, -2.0 / (hself + 1e-06)))
    back = f32(back1) + f32(back3)
    back = back.reshape(around, height, block)
    back_sent = [bf16(back[d]) for d in range(1, around)]
    back_parts = [back[0]] + [f32(moved(v, "dp_0", d)) for d, v in enumerate(back_sent, 1)]
    arrived = after((b0, c0, b1, c1), *back_sent)
    local = own_share() + jnp.concatenate(
        [f32(arrived[0]) + f32(arrived[1]), f32(arrived[2]) + f32(arrived[3])], axis=1
    )
    come1 = after(moved(ckas, "member", 2), *back_sent)[1:2]
    come3 = after(crossing(ckas, -3, -1), *back_sent)[3:4]
    come2 = after(crossing(ckas, 3, 1), *back_sent)[2:3]
    total = own_part + weights[5] * come1
    total = total + either(weights[3], weights[4]) * come3 + either(weights[6], weights[7]) * come2
    self_coef = scale * total
    cka2, held2 = ckas[1:2], ckas[2:3]
    cka1, cka3 = either(come3, held2), either(held2, come3)
    lane = jnp.arange(pairs)[None]
    cka = jnp.where(lane == 0, cka1[:, :pairs], jnp.where(lane == 1, cka2[:, :pairs], cka3[:, :pairs]))

    pieces = [p + self_coef * f32(q) for p, q in zip(back_parts, self_parts)]
    parts = []
    for b in range(around):
        come = pieces[0]
        for d in range(1, around):
            come = jnp.where((x - b) % around == d, pieces[d], come)
        parts.append(math.sqrt(batch) * (local[:, b * block : (b + 1) * block] + come))
    grad = jnp.concatenate(parts, axis=1)
    return (grad[None], cka)


def solution(mesh):
    finer = Mesh(mesh.devices.reshape(mesh.shape["member"], 4, 2), ("member", "dp_0", "dp_1"))
    return jax.shard_map(
        body,
        mesh=finer,
        in_specs=(P("member", DP, None), P()),
        out_specs=(P("member", DP, None), P("member", None)),
        check_vma=False,
    )
```

profile of v0, /device:TPU:23, one launch (start us, length us, event | category | flops | bytes accessed | tf_op | source)
XLA Modules:
  0.0 235.6 jit_solution(12077054368341892963)
XLA Ops:
  0.7 1.5 convert_reduce_fusion
  2.1 0.6 broadcast_in_dim.133
  2.8 4.9 %all-to-all-start = ((f32[8,1,1024]{2,1,0:T(1,128)}), f32[8,1,1024]{2,1,0:T(1,128)S(1)}, u32[]{:S(2)}, u32[]{:S(2)}) async-start(f32[8,1,1024]{2,1,0:T(1,128)} %broadcast_in_dim.133), calls=%async_computation | async-start | bytes 65536 | tf_op jit(solution)/shard_map/all_to_all | solution.py:14
  7.7 2.0 dynamic-slice_bitcast_fusion.2
  10.7 2.4 %collective-permute-start.9 = (bf16[256,1024]{1,0:T(8,128)(2,1)S(1)}, bf16[256,1024]{1,0:T(8,128)(2,1)S(1)}, u32[]{:S(2)}, u32[]{:S(2)}) collective-permute-start(bf16[256,1024]{1,0:T(8,128)(2,1)S(1)} %get-tuple-element.65), channel_id=1, source_target_pairs={{0,2},{2,4},{4,6},{6,0},{1,3},{3,5},{5,7},{7,1},{8,10},{10,12},{12... | collective-permute-start | bytes 1572872 | tf_op jit(solution)/shard_map/ppermute | solution.py:19
  13.1 0.9 collective-permute-start.2
  14.3 3.4 %collective-permute-done = bf16[512,256]{1,0:T(8,128)(2,1)S(1)} collective-permute-done((bf16[512,256]{1,0:T(8,128)(2,1)}, bf16[512,256]{1,0:T(8,128)(2,1)S(1)}, u32[]{:S(2)}, u32[]{:S(2)}) %collective-permute-start) | collective-permute-done | bytes 262176 | tf_op jit(solution)/shard_map/ppermute | solution.py:19
  18.1 11.0 %collective-permute-done.2 = bf16[512,256]{1,0:T(8,128)(2,1)} collective-permute-done((bf16[512,256]{1,0:T(8,128)(2,1)}, bf16[512,256]{1,0:T(8,128)(2,1)}, u32[]{:S(2)}, u32[]{:S(2)}) %collective-permute-start.2) | collective-permute-done | bytes 262176 | tf_op jit(solution)/shard_map/ppermute | solution.py:19
  29.0 3.9 %collective-permute-start.12 = (bf16[256,1024]{1,0:T(8,128)(2,1)S(1)}, bf16[256,1024]{1,0:T(8,128)(2,1)S(1)}, u32[]{:S(2)}, u32[]{:S(2)}) collective-permute-start(bf16[256,1024]{1,0:T(8,128)(2,1)S(1)} %get-tuple-element.64), channel_id=1, source_target_pairs={{0,2},{2,4},{4,6},{6,0},{1,3},{3,5},{5,7},{7,1},{8,10},{10,12},{12... | collective-permute-start | bytes 1572872 | tf_op jit(solution)/shard_map/ppermute | solution.py:19
  33.0 0.6 collective-permute-done.1
  33.6 1.2 fusion.30
  34.8 11.1 %collective-permute-done.8 = bf16[256,1024]{1,0:T(8,128)(2,1)S(1)} collective-permute-done((bf16[256,1024]{1,0:T(8,128)(2,1)S(1)}, bf16[256,1024]{1,0:T(8,128)(2,1)S(1)}, u32[]{:S(2)}, u32[]{:S(2)}) %collective-permute-start.8) | collective-permute-done | bytes 524320 | tf_op jit(solution)/shard_map/ppermute | solution.py:19
  46.1 8.6 %collective-permute-done.10 = bf16[256,1024]{1,0:T(8,128)(2,1)S(1)} collective-permute-done((bf16[256,1024]{1,0:T(8,128)(2,1)S(1)}, bf16[256,1024]{1,0:T(8,128)(2,1)S(1)}, u32[]{:S(2)}, u32[]{:S(2)}) %collective-permute-start.10) | collective-permute-done | bytes 524320 | tf_op jit(solution)/shard_map/ppermute | solution.py:19
  54.7 3.7 %collective-permute-done.11 = bf16[256,1024]{1,0:T(8,128)(2,1)S(1)} collective-permute-done((bf16[256,1024]{1,0:T(8,128)(2,1)S(1)}, bf16[256,1024]{1,0:T(8,128)(2,1)S(1)}, u32[]{:S(2)}, u32[]{:S(2)}) %collective-permute-start.11) | collective-permute-done | bytes 524320 | tf_op jit(solution)/shard_map/ppermute | solution.py:19
  58.8 1.3 convolution_convert_fusion.10
  60.1 0.7 copy-done.5
  60.8 1.2 collective-permute-start.13
  62.0 3.9 %collective-permute-start.3 = (bf16[2048,256]{1,0:T(8,128)(2,1)S(1)}, bf16[2048,256]{1,0:T(8,128)(2,1)S(1)}, u32[]{:S(2)}, u32[]{:S(2)}) collective-permute-start(bf16[2048,256]{1,0:T(8,128)(2,1)S(1)} %pad_maximum_fusion.2), channel_id=1, source_target_pairs={{0,112},{8,120},{16,0},{24,8},{32,16},{40,24},{48,32},{56,40},{64,... | collective-permute-start | bytes 3145736 | tf_op jit(solution)/shard_map/ppermute | solution.py:19
  66.1 1.1 collective-permute-start.5
  67.2 4.1 %collective-permute-done.13 = bf16[1024,256]{1,0:T(8,128)(2,1)S(1)} collective-permute-done((bf16[1024,256]{1,0:T(8,128)(2,1)S(1)}, bf16[1024,256]{1,0:T(8,128)(2,1)S(1)}, u32[]{:S(2)}, u32[]{:S(2)}) %collective-permute-start.13) | collective-permute-done | bytes 524320 | tf_op jit(solution)/shard_map/ppermute | solution.py:19
  72.4 2.5 %collective-permute-done.14 = f32[8,256]{1,0:T(8,128)S(1)} collective-permute-done((f32[8,256]{1,0:T(8,128)S(1)}, f32[8,256]{1,0:T(8,128)S(1)}, u32[]{:S(2)}, u32[]{:S(2)}) %collective-permute-start.14) | collective-permute-done | bytes 8224 | tf_op jit(solution)/shard_map/ppermute | solution.py:100
  75.1 17.6 %collective-permute-done.3 = bf16[2048,256]{1,0:T(8,128)(2,1)S(1)} collective-permute-done((bf16[2048,256]{1,0:T(8,128)(2,1)S(1)}, bf16[2048,256]{1,0:T(8,128)(2,1)S(1)}, u32[]{:S(2)}, u32[]{:S(2)}) %collective-permute-start.3) | collective-permute-done | bytes 1048608 | tf_op jit(solution)/shard_map/ppermute | solution.py:19
  92.8 3.5 %convolution_convert_fusion.9 = bf16[1024,256]{1,0:T(8,128)(2,1)S(1)} fusion(bf16[2048,1024]{1,0:T(8,128)(2,1)} %copy-done.5, bf16[2048,256]{1,0:T(8,128)(2,1)S(1)} %collective-permute-done.3), kind=kOutput, calls=%fused_computation.21 | convolution fusion | flops 1074003968 | bytes 5767168 | tf_op jit(solution)/shard_map/dot_general | solution.py:42
  96.6 4.1 %collective-permute-start.4 = (bf16[2048,256]{1,0:T(8,128)(2,1)S(1)}, bf16[2048,256]{1,0:T(8,128)(2,1)S(1)}, u32[]{:S(2)}, u32[]{:S(2)}) collective-permute-start(bf16[2048,256]{1,0:T(8,128)(2,1)S(1)} %collective-permute-done.3), channel_id=1, source_target_pairs={{0,8},{8,0},{16,24},{24,16},{32,40},{40,32},{48,56},{56,48},{64,72... | collective-permute-start | bytes 3145736 | tf_op jit(solution)/shard_map/ppermute | solution.py:28
  100.7 0.7 collective-permute-start.6
  101.6 6.8 %collective-permute-start.18 = (f32[8,256]{1,0:T(8,128)S(1)}, f32[8,256]{1,0:T(8,128)S(1)}, u32[]{:S(2)}, u32[]{:S(2)}) collective-permute-start(f32[8,256]{1,0:T(8,128)S(1)} %fusion.33), channel_id=1, source_target_pairs={{0,8},{8,32},{16,24},{24,48},{32,40},{40,64},{48,56},{56,80},{64,7... | collective-permute-start | bytes 24584 | tf_op jit(solution)/shard_map/ppermute | solution.py:34
  108.4 1.3 convolution_convert_fusion
  109.8 1.6 collective-permute-start.16
  111.5 1.4 collective-permute-done.17
  113.2 1.3 convolution_convert_fusion.8
  114.5 1.6 collective-permute-start.20
  116.3 1.3 convolution_convert_fusion.7
  117.9 8.1 %collective-permute-done.20 = bf16[1024,256]{1,0:T(8,128)(2,1)S(1)} collective-permute-done((bf16[1024,256]{1,0:T(8,128)(2,1)S(1)}, bf16[1024,256]{1,0:T(8,128)(2,1)S(1)}, u32[]{:S(2)}, u32[]{:S(2)}) %collective-permute-start.20) | collective-permute-done | bytes 524320 | tf_op jit(solution)/shard_map/ppermute | solution.py:19
  126.3 1.3 convolution_convert_fusion.2
  127.6 6.3 %collective-permute-done.21 = bf16[1024,256]{1,0:T(8,128)(2,1)S(1)} collective-permute-done((bf16[1024,256]{1,0:T(8,128)(2,1)S(1)}, bf16[1024,256]{1,0:T(8,128)(2,1)S(1)}, u32[]{:S(2)}, u32[]{:S(2)}) %collective-permute-start.21) | collective-permute-done | bytes 524320 | tf_op jit(solution)/shard_map/ppermute | solution.py:19
  134.2 1.3 convolution_convert_fusion.1
  135.5 8.8 %collective-permute-start.28 = (bf16[2048,256]{1,0:T(8,128)(2,1)S(1)}, bf16[2048,256]{1,0:T(8,128)(2,1)S(1)}, u32[]{:S(2)}, u32[]{:S(2)}) collective-permute-start(bf16[2048,256]{1,0:T(8,128)(2,1)S(1)} %convolution_convert_fusion.2), channel_id=1, source_target_pairs={{0,8},{8,0},{16,24},{24,16},{32,40},{40,32},{48,56},{56,48},{64,72... | collective-permute-start | bytes 3145736 | tf_op jit(solution)/shard_map/ppermute | solution.py:28
  144.4 0.6 convolution_convert_fusion.3
  146.4 0.9 collective-permute-start.33
  147.3 0.6 convolution_convert_fusion.6
  148.0 1.5 collective-permute-start.25
  149.5 1.3 collective-permute-start.27
  150.9 1.1 collective-permute-start.34
  152.0 1.3 fusion
  153.3 4.2 %collective-permute-done.25 = bf16[512,512]{1,0:T(8,128)(2,1)S(1)} collective-permute-done((bf16[512,512]{1,0:T(8,128)(2,1)S(1)}, bf16[512,512]{1,0:T(8,128)(2,1)S(1)}, u32[]{:S(2)}, u32[]{:S(2)}) %collective-permute-start.25) | collective-permute-done | bytes 524320 | tf_op jit(solution)/shard_map/ppermute | solution.py:19
  157.4 2.8 %collective-permute-done.30 = bf16[2048,256]{1,0:T(8,128)(2,1)S(1)} collective-permute-done((bf16[2048,256]{1,0:T(8,128)(2,1)S(1)}, bf16[2048,256]{1,0:T(8,128)(2,1)S(1)}, u32[]{:S(2)}, u32[]{:S(2)}) %collective-permute-start.30) | collective-permute-done | bytes 1048608 | tf_op jit(solution)/shard_map/ppermute | solution.py:19
  160.2 12.8 %collective-permute-start.31 = (bf16[2048,256]{1,0:T(8,128)(2,1)S(1)}, bf16[2048,256]{1,0:T(8,128)(2,1)S(1)}, u32[]{:S(2)}, u32[]{:S(2)}) collective-permute-start(bf16[2048,256]{1,0:T(8,128)(2,1)S(1)} %collective-permute-done.30), channel_id=1, source_target_pairs={{8,120},{24,8},{40,24},{56,40},{72,56},{88,72},{104,88},{120,104},... | collective-permute-start | bytes 3145736 | tf_op jit(solution)/shard_map/ppermute | solution.py:24
  173.0 0.6 fusion.2
  174.3 0.6 fusion.1
  174.9 18.3 %collective-permute-done.37 = f32[8,256]{1,0:T(8,128)S(1)} collective-permute-done((f32[8,256]{1,0:T(8,128)S(1)}, f32[8,256]{1,0:T(8,128)S(1)}, u32[]{:S(2)}, u32[]{:S(2)}) %collective-permute-start.37) | collective-permute-done | bytes 8224 | tf_op jit(solution)/shard_map/ppermute | solution.py:34
  193.2 2.7 %collective-permute-start.23 = (bf16[512,512]{1,0:T(8,128)(2,1)S(1)}, bf16[512,512]{1,0:T(8,128)(2,1)S(1)}, u32[]{:S(2)}, u32[]{:S(2)}) collective-permute-start(bf16[512,512]{1,0:T(8,128)(2,1)S(1)} %fusion.1), channel_id=1, source_target_pairs={{0,2},{2,4},{4,6},{6,0},{1,3},{3,5},{5,7},{7,1},{8,10},{10,12},{12... | collective-permute-start | bytes 1572872 | tf_op jit(solution)/shard_map/ppermute | solution.py:19
  196.4 1.4 collective-permute-done.36
  197.8 6.1 %collective-permute-done.35 = f32[8,256]{1,0:T(8,128)S(1)} collective-permute-done((f32[8,256]{1,0:T(8,128)S(1)}, f32[8,256]{1,0:T(8,128)S(1)}, u32[]{:S(2)}, u32[]{:S(2)}) %collective-permute-start.35) | collective-permute-done | bytes 8224 | tf_op jit(solution)/shard_map/ppermute | solution.py:19
  204.5 1.1 collective-permute-start.40
  205.6 0.7 collective-permute-start.38
  206.3 1.3 collective-permute-done.23
  207.6 0.7 collective-permute-start.32
  208.4 3.9 %collective-permute-start.39 = (bf16[512,256]{1,0:T(8,128)(2,1)S(1)}, bf16[512,256]{1,0:T(8,128)(2,1)S(1)}, u32[]{:S(2)}, u32[]{:S(2)}) collective-permute-start(bf16[512,256]{1,0:T(8,128)(2,1)S(1)} %get-tuple-element.62), channel_id=1, source_target_pairs={{0,4},{2,6},{4,0},{6,2},{1,5},{3,7},{5,1},{7,3},{8,12},{10,14},{12... | collective-permute-start | bytes 786440 | tf_op jit(solution)/shard_map/ppermute | solution.py:19
  212.5 1.0 maximum_add_fusion
  213.5 10.9 %collective-permute-done.42 = bf16[512,256]{1,0:T(8,128)(2,1)S(1)} collective-permute-done((bf16[512,256]{1,0:T(8,128)(2,1)S(1)}, bf16[512,256]{1,0:T(8,128)(2,1)S(1)}, u32[]{:S(2)}, u32[]{:S(2)}) %collective-permute-start.42) | collective-permute-done | bytes 262176 | tf_op jit(solution)/shard_map/ppermute | solution.py:19
  224.5 3.3 %collective-permute-start.41 = (bf16[512,256]{1,0:T(8,128)(2,1)S(1)}, bf16[512,256]{1,0:T(8,128)(2,1)S(1)}, u32[]{:S(2)}, u32[]{:S(2)}) collective-permute-start(bf16[512,256]{1,0:T(8,128)(2,1)S(1)} %get-tuple-element.63), channel_id=1, source_target_pairs={{0,2},{2,4},{4,6},{6,0},{1,3},{3,5},{5,7},{7,1},{8,10},{10,12},{12... | collective-permute-start | bytes 786440 | tf_op jit(solution)/shard_map/ppermute | solution.py:19
  228.4 2.4 %collective-permute-done.39 = bf16[512,256]{1,0:T(8,128)(2,1)S(1)} collective-permute-done((bf16[512,256]{1,0:T(8,128)(2,1)S(1)}, bf16[512,256]{1,0:T(8,128)(2,1)S(1)}, u32[]{:S(2)}, u32[]{:S(2)}) %collective-permute-start.39) | collective-permute-done | bytes 262176 | tf_op jit(solution)/shard_map/ppermute | solution.py:19
  230.8 2.3 collective-permute-done.41
  234.0 1.6 maximum_bitcast_fusion
  (106 shorter events, 10.8 us)
Async XLA Ops:
  0.6 9.7 %copy-start = (bf16[1,512,1024]{2,1,0:T(8,128)(2,1)S(1)}, bf16[1,512,1024]{2,1,0:T(8,128)(2,1)}, u32[]{:S(2)}) copy-start(bf16[1,512,1024]{2,1,0:T(8,128)(2,1)} %param.2) | copy-start | bytes 3145732
  0.6 13.4 %copy-start.7 = (f32[16,3]{0,1:T(4,128)S(1)}, f32[16,3]{0,1:T(4,128)}, u32[]{:S(2)}) copy-start(f32[16,3]{0,1:T(4,128)} %param.3) | copy-start | bytes 580
  2.8 11.5 %all-to-all-start = ((f32[8,1,1024]{2,1,0:T(1,128)}), f32[8,1,1024]{2,1,0:T(1,128)S(1)}, u32[]{:S(2)}, u32[]{:S(2)}) async-start(f32[8,1,1024]{2,1,0:T(1,128)} %broadcast_in_dim.133), calls=%async_computation | async-start | bytes 65536 | tf_op jit(solution)/shard_map/all_to_all | solution.py:14
  9.7 8.0 %collective-permute-start = (bf16[512,256]{1,0:T(8,128)(2,1)}, bf16[512,256]{1,0:T(8,128)(2,1)S(1)}, u32[]{:S(2)}, u32[]{:S(2)}) collective-permute-start(bf16[512,256]{1,0:T(8,128)(2,1)} %get-tuple-element.66), channel_id=1, source_target_pairs={{0,6},{2,0},{4,2},{6,4},{1,7},{3,1},{5,3},{7,5},{8,14},{10,8},{12,... | collective-permute-start | bytes 786440 | tf_op jit(solution)/shard_map/ppermute | solution.py:19
  10.4 35.5 %collective-permute-start.7 = (bf16[256,1024]{1,0:T(8,128)(2,1)S(1)}, bf16[256,1024]{1,0:T(8,128)(2,1)S(1)}, u32[]{:S(2)}, u32[]{:S(2)}) collective-permute-start(bf16[256,1024]{1,0:T(8,128)(2,1)S(1)} %get-tuple-element.65), channel_id=1, source_target_pairs={{0,6},{2,0},{4,2},{6,4},{1,7},{3,1},{5,3},{7,5},{8,14},{10,8},{12,... | collective-permute-start | bytes 1572872 | tf_op jit(solution)/shard_map/ppermute | solution.py:19
  10.7 22.2 %collective-permute-start.9 = (bf16[256,1024]{1,0:T(8,128)(2,1)S(1)}, bf16[256,1024]{1,0:T(8,128)(2,1)S(1)}, u32[]{:S(2)}, u32[]{:S(2)}) collective-permute-start(bf16[256,1024]{1,0:T(8,128)(2,1)S(1)} %get-tuple-element.65), channel_id=1, source_target_pairs={{0,2},{2,4},{4,6},{6,0},{1,3},{3,5},{5,7},{7,1},{8,10},{10,12},{12... | collective-permute-start | bytes 1572872 | tf_op jit(solution)/shard_map/ppermute | solution.py:19
  13.1 15.9 %collective-permute-start.2 = (bf16[512,256]{1,0:T(8,128)(2,1)}, bf16[512,256]{1,0:T(8,128)(2,1)}, u32[]{:S(2)}, u32[]{:S(2)}) collective-permute-start(bf16[512,256]{1,0:T(8,128)(2,1)} %get-tuple-element.67), channel_id=1, source_target_pairs={{0,2},{2,4},{4,6},{6,0},{1,3},{3,5},{5,7},{7,1},{8,10},{10,12},{12... | collective-permute-start | bytes 786440 | tf_op jit(solution)/shard_map/ppermute | solution.py:19
  14.0 19.6 %collective-permute-start.1 = (bf16[512,256]{1,0:T(8,128)(2,1)}, bf16[512,256]{1,0:T(8,128)(2,1)}, u32[]{:S(2)}, u32[]{:S(2)}) collective-permute-start(bf16[512,256]{1,0:T(8,128)(2,1)} %get-tuple-element.68), channel_id=1, source_target_pairs={{0,4},{2,6},{4,0},{6,2},{1,5},{3,7},{5,1},{7,3},{8,12},{10,14},{12... | collective-permute-start | bytes 786440 | tf_op jit(solution)/shard_map/ppermute | solution.py:19
  17.8 28.1 %collective-permute-start.8 = (bf16[256,1024]{1,0:T(8,128)(2,1)S(1)}, bf16[256,1024]{1,0:T(8,128)(2,1)S(1)}, u32[]{:S(2)}, u32[]{:S(2)}) collective-permute-start(bf16[256,1024]{1,0:T(8,128)(2,1)S(1)} %get-tuple-element.64), channel_id=1, source_target_pairs={{0,6},{2,0},{4,2},{6,4},{1,7},{3,1},{5,3},{7,5},{8,14},{10,8},{12,... | collective-permute-start | bytes 1572872 | tf_op jit(solution)/shard_map/ppermute | solution.py:19
  29.0 29.6 %collective-permute-start.12 = (bf16[256,1024]{1,0:T(8,128)(2,1)S(1)}, bf16[256,1024]{1,0:T(8,128)(2,1)S(1)}, u32[]{:S(2)}, u32[]{:S(2)}) collective-permute-start(bf16[256,1024]{1,0:T(8,128)(2,1)S(1)} %get-tuple-element.64), channel_id=1, source_target_pairs={{0,2},{2,4},{4,6},{6,0},{1,3},{3,5},{5,7},{7,1},{8,10},{10,12},{12... | collective-permute-start | bytes 1572872 | tf_op jit(solution)/shard_map/ppermute | solution.py:19
  32.9 21.7 %collective-permute-start.10 = (bf16[256,1024]{1,0:T(8,128)(2,1)S(1)}, bf16[256,1024]{1,0:T(8,128)(2,1)S(1)}, u32[]{:S(2)}, u32[]{:S(2)}) collective-permute-start(bf16[256,1024]{1,0:T(8,128)(2,1)S(1)} %collective-permute-done.9), channel_id=1, source_target_pairs={{0,2},{2,4},{4,6},{6,0},{1,3},{3,5},{5,7},{7,1},{8,10},{10,12},{12... | collective-permute-start | bytes 1572872 | tf_op jit(solution)/shard_map/ppermute | solution.py:19
  45.9 12.6 %collective-permute-start.11 = (bf16[256,1024]{1,0:T(8,128)(2,1)S(1)}, bf16[256,1024]{1,0:T(8,128)(2,1)S(1)}, u32[]{:S(2)}, u32[]{:S(2)}) collective-permute-start(bf16[256,1024]{1,0:T(8,128)(2,1)S(1)} %collective-permute-done.8), channel_id=1, source_target_pairs={{0,6},{2,0},{4,2},{6,4},{1,7},{3,1},{5,3},{7,5},{8,14},{10,8},{12,... | collective-permute-start | bytes 1572872 | tf_op jit(solution)/shard_map/ppermute | solution.py:19
  58.8 2.0 copy-start.5
  60.8 10.5 %copy-start.1 = (bf16[1024,256]{1,0:T(8,128)(2,1)}, bf16[1024,256]{1,0:T(8,128)(2,1)S(1)}, u32[]{:S(2)}) copy-start(bf16[1024,256]{1,0:T(8,128)(2,1)S(1)} %convolution_convert_fusion.10) | copy-start | bytes 1572868
  60.8 10.5 %collective-permute-start.13 = (bf16[1024,256]{1,0:T(8,128)(2,1)S(1)}, bf16[1024,256]{1,0:T(8,128)(2,1)S(1)}, u32[]{:S(2)}, u32[]{:S(2)}) collective-permute-start(bf16[1024,256]{1,0:T(8,128)(2,1)S(1)} %convolution_convert_fusion.10), channel_id=1, source_target_pairs={{0,1},{1,0},{2,3},{3,2},{4,5},{5,4},{6,7},{7,6},{8,9},{9,8},{10,11... | collective-permute-start | bytes 1572872 | tf_op jit(solution)/shard_map/ppermute | solution.py:19
  62.0 30.7 %collective-permute-start.3 = (bf16[2048,256]{1,0:T(8,128)(2,1)S(1)}, bf16[2048,256]{1,0:T(8,128)(2,1)S(1)}, u32[]{:S(2)}, u32[]{:S(2)}) collective-permute-start(bf16[2048,256]{1,0:T(8,128)(2,1)S(1)} %pad_maximum_fusion.2), channel_id=1, source_target_pairs={{0,112},{8,120},{16,0},{24,8},{32,16},{40,24},{48,32},{56,40},{64,... | collective-permute-start | bytes 3145736 | tf_op jit(solution)/shard_map/ppermute | solution.py:19
  66.1 34.6 %collective-permute-start.5 = (bf16[2048,256]{1,0:T(8,128)(2,1)S(1)}, bf16[2048,256]{1,0:T(8,128)(2,1)S(1)}, u32[]{:S(2)}, u32[]{:S(2)}) collective-permute-start(bf16[2048,256]{1,0:T(8,128)(2,1)S(1)} %pad_maximum_fusion.2), channel_id=1, source_target_pairs={{0,8},{8,16},{16,24},{24,32},{32,40},{40,48},{48,56},{56,64},{64,7... | collective-permute-start | bytes 3145736 | tf_op jit(solution)/shard_map/ppermute | solution.py:19
  71.3 0.8 copy-start.3
  72.2 2.8 %collective-permute-start.14 = (f32[8,256]{1,0:T(8,128)S(1)}, f32[8,256]{1,0:T(8,128)S(1)}, u32[]{:S(2)}, u32[]{:S(2)}) collective-permute-start(f32[8,256]{1,0:T(8,128)S(1)} %broadcast_select_fusion.1), channel_id=1, source_target_pairs={{0,2},{2,0},{4,6},{6,4},{1,3},{3,1},{5,7},{7,5},{8,10},{10,8},{12,... | collective-permute-start | bytes 24584 | tf_op jit(solution)/shard_map/ppermute | solution.py:100
  75.0 33.3 %copy-start.2 = (bf16[1024,256]{1,0:T(8,128)(2,1)S(1)}, bf16[1024,256]{1,0:T(8,128)(2,1)}, u32[]{:S(2)}) copy-start(bf16[1024,256]{1,0:T(8,128)(2,1)} %copy-done.1) | copy-start | bytes 1572868
  75.0 33.3 %copy-start.4 = (bf16[1024,256]{1,0:T(8,128)(2,1)S(1)}, bf16[1024,256]{1,0:T(8,128)(2,1)}, u32[]{:S(2)}) copy-start(bf16[1024,256]{1,0:T(8,128)(2,1)} %copy-done.3) | copy-start | bytes 1572868
  75.0 33.3 %copy-start.6 = (bf16[2048,1024]{1,0:T(8,128)(2,1)S(1)}, bf16[2048,1024]{1,0:T(8,128)(2,1)}, u32[]{:S(2)}) copy-start(bf16[2048,1024]{1,0:T(8,128)(2,1)} %copy-done.5) | copy-start | bytes 12582916
  75.0 26.4 %collective-permute-start.15 = (f32[8,256]{1,0:T(8,128)S(1)}, f32[8,256]{1,0:T(8,128)S(1)}, u32[]{:S(2)}, u32[]{:S(2)}) collective-permute-start(f32[8,256]{1,0:T(8,128)S(1)} %fusion.37), channel_id=1, source_target_pairs={{0,4},{2,6},{4,0},{6,2},{1,5},{3,7},{5,1},{7,3},{8,12},{10,14},{12... | collective-permute-start | bytes 24584 | tf_op jit(solution)/shard_map/ppermute | solution.py:100
  96.2 16.6 %collective-permute-start.19 = (bf16[1024,256]{1,0:T(8,128)(2,1)S(1)}, bf16[1024,256]{1,0:T(8,128)(2,1)S(1)}, u32[]{:S(2)}, u32[]{:S(2)}) collective-permute-start(bf16[1024,256]{1,0:T(8,128)(2,1)S(1)} %convolution_convert_fusion.9), channel_id=1, source_target_pairs={{0,1},{1,0},{2,3},{3,2},{4,5},{5,4},{6,7},{7,6},{8,9},{9,8},{10,11... | collective-permute-start | bytes 1572872 | tf_op jit(solution)/shard_map/ppermute | solution.py:19
  96.6 16.6 %collective-permute-start.4 = (bf16[2048,256]{1,0:T(8,128)(2,1)S(1)}, bf16[2048,256]{1,0:T(8,128)(2,1)S(1)}, u32[]{:S(2)}, u32[]{:S(2)}) collective-permute-start(bf16[2048,256]{1,0:T(8,128)(2,1)S(1)} %collective-permute-done.3), channel_id=1, source_target_pairs={{0,8},{8,0},{16,24},{24,16},{32,40},{40,32},{48,56},{56,48},{64,72... | collective-permute-start | bytes 3145736 | tf_op jit(solution)/shard_map/ppermute | solution.py:28
  100.7 15.4 %collective-permute-start.6 = (bf16[2048,256]{1,0:T(8,128)(2,1)S(1)}, bf16[2048,256]{1,0:T(8,128)(2,1)S(1)}, u32[]{:S(2)}, u32[]{:S(2)}) collective-permute-start(bf16[2048,256]{1,0:T(8,128)(2,1)S(1)} %collective-permute-done.5), channel_id=1, source_target_pairs={{0,16},{16,32},{32,48},{48,64},{64,80},{80,96},{96,112},{112,0},{1... | collective-permute-start | bytes 3145736 | tf_op jit(solution)/shard_map/ppermute | solution.py:24
  101.6 8.2 %collective-permute-start.18 = (f32[8,256]{1,0:T(8,128)S(1)}, f32[8,256]{1,0:T(8,128)S(1)}, u32[]{:S(2)}, u32[]{:S(2)}) collective-permute-start(f32[8,256]{1,0:T(8,128)S(1)} %fusion.33), channel_id=1, source_target_pairs={{0,8},{8,32},{16,24},{24,48},{32,40},{40,64},{48,56},{56,80},{64,7... | collective-permute-start | bytes 24584 | tf_op jit(solution)/shard_map/ppermute | solution.py:34
  109.7 3.1 %collective-permute-start.17 = (f32[8,256]{1,0:T(8,128)S(1)}, f32[8,256]{1,0:T(8,128)S(1)}, u32[]{:S(2)}, u32[]{:S(2)}) collective-permute-start(f32[8,256]{1,0:T(8,128)S(1)} %fusion.33), channel_id=1, source_target_pairs={{0,120},{8,112},{16,8},{24,0},{32,24},{40,16},{48,40},{56,32},{64,... | collective-permute-start | bytes 24584 | tf_op jit(solution)/shard_map/ppermute | solution.py:34
  109.8 3.1 %collective-permute-start.16 = (f32[8,256]{1,0:T(8,128)S(1)}, f32[8,256]{1,0:T(8,128)S(1)}, u32[]{:S(2)}, u32[]{:S(2)}) collective-permute-start(f32[8,256]{1,0:T(8,128)S(1)} %fusion.33), channel_id=1, source_target_pairs={{0,112},{8,120},{16,0},{24,8},{32,16},{40,24},{48,32},{56,40},{64,... | collective-permute-start | bytes 24584 | tf_op jit(solution)/shard_map/ppermute | solution.py:19
  114.5 11.6 %collective-permute-start.20 = (bf16[1024,256]{1,0:T(8,128)(2,1)S(1)}, bf16[1024,256]{1,0:T(8,128)(2,1)S(1)}, u32[]{:S(2)}, u32[]{:S(2)}) collective-permute-start(bf16[1024,256]{1,0:T(8,128)(2,1)S(1)} %convolution_convert_fusion.8), channel_id=1, source_target_pairs={{0,1},{1,0},{2,3},{3,2},{4,5},{5,4},{6,7},{7,6},{8,9},{9,8},{10,11... | collective-permute-start | bytes 1572872 | tf_op jit(solution)/shard_map/ppermute | solution.py:19
  117.6 16.4 %collective-permute-start.21 = (bf16[1024,256]{1,0:T(8,128)(2,1)S(1)}, bf16[1024,256]{1,0:T(8,128)(2,1)S(1)}, u32[]{:S(2)}, u32[]{:S(2)}) collective-permute-start(bf16[1024,256]{1,0:T(8,128)(2,1)S(1)} %convolution_convert_fusion.7), channel_id=1, source_target_pairs={{0,1},{1,0},{2,3},{3,2},{4,5},{5,4},{6,7},{7,6},{8,9},{9,8},{10,11... | collective-permute-start | bytes 1572872 | tf_op jit(solution)/shard_map/ppermute | solution.py:19
  135.5 15.4 %collective-permute-start.28 = (bf16[2048,256]{1,0:T(8,128)(2,1)S(1)}, bf16[2048,256]{1,0:T(8,128)(2,1)S(1)}, u32[]{:S(2)}, u32[]{:S(2)}) collective-permute-start(bf16[2048,256]{1,0:T(8,128)(2,1)S(1)} %convolution_convert_fusion.2), channel_id=1, source_target_pairs={{0,8},{8,0},{16,24},{24,16},{32,40},{40,32},{48,56},{56,48},{64,72... | collective-permute-start | bytes 3145736 | tf_op jit(solution)/shard_map/ppermute | solution.py:28
  145.6 14.6 %collective-permute-start.30 = (bf16[2048,256]{1,0:T(8,128)(2,1)S(1)}, bf16[2048,256]{1,0:T(8,128)(2,1)S(1)}, u32[]{:S(2)}, u32[]{:S(2)}) collective-permute-start(bf16[2048,256]{1,0:T(8,128)(2,1)S(1)} %convolution_convert_fusion.1), channel_id=1, source_target_pairs={{0,120},{8,0},{16,8},{24,16},{32,24},{40,32},{48,40},{56,48},{64,5... | collective-permute-start | bytes 3145736 | tf_op jit(solution)/shard_map/ppermute | solution.py:19
  146.4 3.1 %collective-permute-start.33 = (f32[8,256]{1,0:T(8,128)S(1)}, f32[8,256]{1,0:T(8,128)S(1)}, u32[]{:S(2)}, u32[]{:S(2)}) collective-permute-start(f32[8,256]{1,0:T(8,128)S(1)} %select_add_fusion), channel_id=1, source_target_pairs={{0,2},{2,0},{4,6},{6,4},{1,3},{3,1},{5,7},{7,5},{8,10},{10,8},{12,... | collective-permute-start | bytes 24584 | tf_op jit(solution)/shard_map/ppermute | solution.py:100
  147.9 26.3 %collective-permute-start.22 = (bf16[512,512]{1,0:T(8,128)(2,1)S(1)}, bf16[512,512]{1,0:T(8,128)(2,1)S(1)}, u32[]{:S(2)}, u32[]{:S(2)}) collective-permute-start(bf16[512,512]{1,0:T(8,128)(2,1)S(1)} %convolution_convert_fusion.6), channel_id=1, source_target_pairs={{0,2},{2,4},{4,6},{6,0},{1,3},{3,5},{5,7},{7,1},{8,10},{10,12},{12... | collective-permute-start | bytes 1572872 | tf_op jit(solution)/shard_map/ppermute | solution.py:19
  148.0 9.4 %collective-permute-start.25 = (bf16[512,512]{1,0:T(8,128)(2,1)S(1)}, bf16[512,512]{1,0:T(8,128)(2,1)S(1)}, u32[]{:S(2)}, u32[]{:S(2)}) collective-permute-start(bf16[512,512]{1,0:T(8,128)(2,1)S(1)} %convolution_convert_fusion.4), channel_id=1, source_target_pairs={{0,6},{2,0},{4,2},{6,4},{1,7},{3,1},{5,3},{7,5},{8,14},{10,8},{12,... | collective-permute-start | bytes 1572872 | tf_op jit(solution)/shard_map/ppermute | solution.py:19
  149.5 56.1 %collective-permute-start.27 = (bf16[512,512]{1,0:T(8,128)(2,1)S(1)}, bf16[512,512]{1,0:T(8,128)(2,1)S(1)}, u32[]{:S(2)}, u32[]{:S(2)}) collective-permute-start(bf16[512,512]{1,0:T(8,128)(2,1)S(1)} %convolution_convert_fusion.3), channel_id=1, source_target_pairs={{0,2},{2,4},{4,6},{6,0},{1,3},{3,5},{5,7},{7,1},{8,10},{10,12},{12... | collective-permute-start | bytes 1572872 | tf_op jit(solution)/shard_map/ppermute | solution.py:19
  150.9 22.8 %collective-permute-start.34 = (f32[8,256]{1,0:T(8,128)S(1)}, f32[8,256]{1,0:T(8,128)S(1)}, u32[]{:S(2)}, u32[]{:S(2)}) collective-permute-start(f32[8,256]{1,0:T(8,128)S(1)} %fusion.52), channel_id=1, source_target_pairs={{0,4},{2,6},{4,0},{6,2},{1,5},{3,7},{5,1},{7,3},{8,12},{10,14},{12... | collective-permute-start | bytes 24584 | tf_op jit(solution)/shard_map/ppermute | solution.py:100
  157.4 35.8 %collective-permute-start.29 = (bf16[2048,256]{1,0:T(8,128)(2,1)S(1)}, bf16[2048,256]{1,0:T(8,128)(2,1)S(1)}, u32[]{:S(2)}, u32[]{:S(2)}) collective-permute-start(bf16[2048,256]{1,0:T(8,128)(2,1)S(1)} %fusion), channel_id=1, source_target_pairs={{0,16},{8,24},{16,32},{24,40},{32,48},{40,56},{48,64},{56,72},{64,... | collective-permute-start | bytes 3145736 | tf_op jit(solution)/shard_map/ppermute | solution.py:19
  160.2 33.0 %collective-permute-start.31 = (bf16[2048,256]{1,0:T(8,128)(2,1)S(1)}, bf16[2048,256]{1,0:T(8,128)(2,1)S(1)}, u32[]{:S(2)}, u32[]{:S(2)}) collective-permute-start(bf16[2048,256]{1,0:T(8,128)(2,1)S(1)} %collective-permute-done.30), channel_id=1, source_target_pairs={{8,120},{24,8},{40,24},{56,40},{72,56},{88,72},{104,88},{120,104},... | collective-permute-start | bytes 3145736 | tf_op jit(solution)/shard_map/ppermute | solution.py:24
  173.7 30.8 %collective-permute-start.24 = (bf16[512,512]{1,0:T(8,128)(2,1)S(1)}, bf16[512,512]{1,0:T(8,128)(2,1)S(1)}, u32[]{:S(2)}, u32[]{:S(2)}) collective-permute-start(bf16[512,512]{1,0:T(8,128)(2,1)S(1)} %convolution_convert_fusion.5), channel_id=1, source_target_pairs={{0,6},{2,0},{4,2},{6,4},{1,7},{3,1},{5,3},{7,5},{8,14},{10,8},{12,... | collective-permute-start | bytes 1572872 | tf_op jit(solution)/shard_map/ppermute | solution.py:19
  174.2 19.0 %collective-permute-start.37 = (f32[8,256]{1,0:T(8,128)S(1)}, f32[8,256]{1,0:T(8,128)S(1)}, u32[]{:S(2)}, u32[]{:S(2)}) collective-permute-start(f32[8,256]{1,0:T(8,128)S(1)} %select_select_fusion), channel_id=1, source_target_pairs={{0,24},{8,16},{16,40},{24,32},{32,56},{40,48},{48,72},{56,64},{64,... | collective-permute-start | bytes 24584 | tf_op jit(solution)/shard_map/ppermute | solution.py:34
  193.2 4.6 %collective-permute-start.36 = (f32[8,256]{1,0:T(8,128)S(1)}, f32[8,256]{1,0:T(8,128)S(1)}, u32[]{:S(2)}, u32[]{:S(2)}) collective-permute-start(f32[8,256]{1,0:T(8,128)S(1)} %select_select_fusion), channel_id=1, source_target_pairs={{0,104},{8,0},{16,120},{24,16},{32,8},{40,32},{48,24},{56,48},{64,... | collective-permute-start | bytes 24584 | tf_op jit(solution)/shard_map/ppermute | solution.py:34
  193.2 15.2 %collective-permute-start.26 = (bf16[512,512]{1,0:T(8,128)(2,1)S(1)}, bf16[512,512]{1,0:T(8,128)(2,1)S(1)}, u32[]{:S(2)}, u32[]{:S(2)}) collective-permute-start(bf16[512,512]{1,0:T(8,128)(2,1)S(1)} %fusion.2), channel_id=1, source_target_pairs={{0,6},{2,0},{4,2},{6,4},{1,7},{3,1},{5,3},{7,5},{8,14},{10,8},{12,... | collective-permute-start | bytes 1572872 | tf_op jit(solution)/shard_map/ppermute | solution.py:19
  193.2 14.4 %collective-permute-start.23 = (bf16[512,512]{1,0:T(8,128)(2,1)S(1)}, bf16[512,512]{1,0:T(8,128)(2,1)S(1)}, u32[]{:S(2)}, u32[]{:S(2)}) collective-permute-start(bf16[512,512]{1,0:T(8,128)(2,1)S(1)} %fusion.1), channel_id=1, source_target_pairs={{0,2},{2,4},{4,6},{6,0},{1,3},{3,5},{5,7},{7,1},{8,10},{10,12},{12... | collective-permute-start | bytes 1572872 | tf_op jit(solution)/shard_map/ppermute | solution.py:19
  197.8 6.1 %collective-permute-start.35 = (f32[8,256]{1,0:T(8,128)S(1)}, f32[8,256]{1,0:T(8,128)S(1)}, u32[]{:S(2)}, u32[]{:S(2)}) collective-permute-start(f32[8,256]{1,0:T(8,128)S(1)} %select_select_fusion), channel_id=1, source_target_pairs={{0,16},{8,24},{16,32},{24,40},{32,48},{40,56},{48,64},{56,72},{64,... | collective-permute-start | bytes 24584 | tf_op jit(solution)/shard_map/ppermute | solution.py:19
  203.9 20.6 %collective-permute-start.42 = (bf16[512,256]{1,0:T(8,128)(2,1)S(1)}, bf16[512,256]{1,0:T(8,128)(2,1)S(1)}, u32[]{:S(2)}, u32[]{:S(2)}) collective-permute-start(bf16[512,256]{1,0:T(8,128)(2,1)S(1)} %get-tuple-element.58), channel_id=1, source_target_pairs={{0,2},{2,4},{4,6},{6,0},{1,3},{3,5},{5,7},{7,1},{8,10},{10,12},{12... | collective-permute-start | bytes 786440 | tf_op jit(solution)/shard_map/ppermute | solution.py:19
  204.5 23.9 %collective-permute-start.40 = (bf16[512,256]{1,0:T(8,128)(2,1)S(1)}, bf16[512,256]{1,0:T(8,128)(2,1)S(1)}, u32[]{:S(2)}, u32[]{:S(2)}) collective-permute-start(bf16[512,256]{1,0:T(8,128)(2,1)S(1)} %get-tuple-element.59), channel_id=1, source_target_pairs={{0,4},{2,6},{4,0},{6,2},{1,5},{3,7},{5,1},{7,3},{8,12},{10,14},{12... | collective-permute-start | bytes 786440 | tf_op jit(solution)/shard_map/ppermute | solution.py:19
  205.6 22.8 %collective-permute-start.38 = (bf16[512,256]{1,0:T(8,128)(2,1)S(1)}, bf16[512,256]{1,0:T(8,128)(2,1)S(1)}, u32[]{:S(2)}, u32[]{:S(2)}) collective-permute-start(bf16[512,256]{1,0:T(8,128)(2,1)S(1)} %get-tuple-element.60), channel_id=1, source_target_pairs={{0,6},{2,0},{4,2},{6,4},{1,7},{3,1},{5,3},{7,5},{8,14},{10,8},{12,... | collective-permute-start | bytes 786440 | tf_op jit(solution)/shard_map/ppermute | solution.py:19
  207.6 20.7 %collective-permute-start.32 = (bf16[512,256]{1,0:T(8,128)(2,1)S(1)}, bf16[512,256]{1,0:T(8,128)(2,1)S(1)}, u32[]{:S(2)}, u32[]{:S(2)}) collective-permute-start(bf16[512,256]{1,0:T(8,128)(2,1)S(1)} %get-tuple-element.61), channel_id=1, source_target_pairs={{0,6},{2,0},{4,2},{6,4},{1,7},{3,1},{5,3},{7,5},{8,14},{10,8},{12,... | collective-permute-start | bytes 786440 | tf_op jit(solution)/shard_map/ppermute | solution.py:19
  208.4 22.4 %collective-permute-start.39 = (bf16[512,256]{1,0:T(8,128)(2,1)S(1)}, bf16[512,256]{1,0:T(8,128)(2,1)S(1)}, u32[]{:S(2)}, u32[]{:S(2)}) collective-permute-start(bf16[512,256]{1,0:T(8,128)(2,1)S(1)} %get-tuple-element.62), channel_id=1, source_target_pairs={{0,4},{2,6},{4,0},{6,2},{1,5},{3,7},{5,1},{7,3},{8,12},{10,14},{12... | collective-permute-start | bytes 786440 | tf_op jit(solution)/shard_map/ppermute | solution.py:19
  224.5 8.6 %collective-permute-start.41 = (bf16[512,256]{1,0:T(8,128)(2,1)S(1)}, bf16[512,256]{1,0:T(8,128)(2,1)S(1)}, u32[]{:S(2)}, u32[]{:S(2)}) collective-permute-start(bf16[512,256]{1,0:T(8,128)(2,1)S(1)} %get-tuple-element.63), channel_id=1, source_target_pairs={{0,2},{2,4},{4,6},{6,0},{1,3},{3,5},{5,7},{7,1},{8,10},{10,12},{12... | collective-permute-start | bytes 786440 | tf_op jit(solution)/shard_map/ppermute | solution.py:19
where the time goes:
time: 240 us; the launch traced here: 236 us
  waiting for transfers between devices  128 us (53%)
  starting transfers between devices  74.8 us (31%)
  matrix products  17.5 us (7%)
  other arithmetic  9.58 us (4%)
  local copies, waits for them, and re-layouts  4.46 us (2%)
    ppermute x31, waiting for transfers between devices, moved(): lax.ppermute(value, axis, [(s, (s + steps) % count) for s in range(count)])  105 us
    ppermute x31, starting transfers between devices, moved(): lax.ppermute(value, axis, [(s, (s + steps) % count) for s in range(count)])  34.2 us
    ppermute x4, waiting for transfers between devices, crossing(): return lax.ppermute(value, 'member', pairs)  21.1 us
    dot_general x15, matrix products, wide_dot(): lax.dot_general(a, b, (((left,), (right,)), ((), ())), preferred_element_...  17.2 us
    ppermute x2, starting transfers between devices, moved_some(): lax.ppermute(value, 'member', [(s, (s + steps) % count) for s in range(fi...  13.5 us
    ppermute x2, starting transfers between devices, swapped(): lax.ppermute(value, 'member', [(s, s ^ 1) for s in range(lax.axis_size('m...  12.9 us
    ppermute x4, starting transfers between devices, crossing(): return lax.ppermute(value, 'member', pairs)  6.89 us
    all_to_all x1, starting transfers between devices, of_everyone(): return lax.all_to_all(copies, axis, split_axis=0, concat_axis=0, tiled=True)  4.93 us
  transfers between devices with their start and end apart: 44, of which 21 were waited for; matrix products, arithmetic and copies ran while one was open for 10% of the time, Pallas kernels for 0%

commit v1 on v0

--- a/solution.py
+++ b/solution.py
@@ -199,12 +199,14 @@
     lane = jnp.arange(pairs)[None]
     cka = jnp.where(lane == 0, cka1[:, :pairs], jnp.where(lane == 1, cka2[:, :pairs], cka3[:, :pairs]))
 
-    pieces = [p + self_coef * f32(q) for p, q in zip(back_parts, self_parts)]
     parts = []
     for b in range(around):
-        come = pieces[0]
+        come, own_come = back_parts[0], self_parts[0]
         for d in range(1, around):
-            come = jnp.where((x - b) % around == d, pieces[d], come)
+            here = (x - b) % around == d
+            come = jnp.where(here, back_parts[d], come)
+            own_come = jnp.where(here, self_parts[d], own_come)
+        come = come + self_coef * f32(own_come)
         parts.append(math.sqrt(batch) * (local[:, b * block : (b + 1) * block] + come))
     grad = jnp.concatenate(parts, axis=1)
     return (grad[None], cka)

time: 240 us -> 215 us (0.90)
  the two profiles are of different devices: /device:TPU:23 before, /device:TPU:0 now
where the time goes in v1:
time: 215 us
  waiting for transfers between devices  112 us (52%)
  starting transfers between devices  70.4 us (33%)
  matrix products  17.8 us (8%)
  other arithmetic  8.36 us (4%)
  local copies, waits for them, and re-layouts  4.97 us (2%)
    ppermute x31, waiting for transfers between devices, moved(): lax.ppermute(value, axis, [(s, (s + steps) % count) for s in range(count)])  82.9 us
    ppermute x31, starting transfers between devices, moved(): lax.ppermute(value, axis, [(s, (s + steps) % count) for s in range(count)])  53.5 us
    dot_general x15, matrix products, wide_dot(): lax.dot_general(a, b, (((left,), (right,)), ((), ())), preferred_element_...  17.5 us
    ppermute x4, waiting for transfers between devices, over_ring(): come = lax.ppermute(value, 'dp_0', [(s, s ^ bit) for s in range(around)])  12.1 us
    all_to_all x1, waiting for transfers between devices, of_everyone(): return lax.all_to_all(copies, axis, split_axis=0, concat_axis=0, tiled=True)  8.89 us
    ppermute x2, waiting for transfers between devices, moved_some(): lax.ppermute(value, 'member', [(s, (s + steps) % count) for s in range(fi...  7.27 us
    ppermute x4, starting transfers between devices, crossing(): return lax.ppermute(value, 'member', pairs)  5.69 us
    all_to_all x1, starting transfers between devices, of_everyone(): return lax.all_to_all(copies, axis, split_axis=0, concat_axis=0, tiled=True)  5.52 us
  transfers between devices with their start and end apart: 44, of which 22 were waited for; matrix products, arithmetic and copies ran while one was open for 11% of the time, Pallas kernels for 0%

profile of v1, /device:TPU:0, one launch (start us, length us, event | category | flops | bytes accessed | tf_op | source)
XLA Modules:
  0.0 214.7 jit_solution(10876832375276668664)
XLA Ops:
  0.6 2.3 %slice_bitcast_fusion = (bf16[256,1024]{1,0:T(8,128)(2,1)}, bf16[256,1024]{1,0:T(8,128)(2,1)}) fusion(bf16[1,512,1024]{2,1,0:T(8,128)(2,1)} %param.2), kind=kLoop, calls=%fused_computation.94 | loop fusion | bytes 2097152 | tf_op jit(solution)/shard_map/slice | solution.py:83
  3.0 2.9 %collective-permute-start.7 = (bf16[256,1024]{1,0:T(8,128)(2,1)}, bf16[256,1024]{1,0:T(8,128)(2,1)S(1)}, u32[]{:S(2)}, u32[]{:S(2)}) collective-permute-start(bf16[256,1024]{1,0:T(8,128)(2,1)} %get-tuple-element.68), channel_id=1, source_target_pairs={{0,6},{2,0},{4,2},{6,4},{1,7},{3,1},{5,3},{7,5},{8,14},{10,8},{12,... | collective-permute-start | bytes 1572872 | tf_op jit(solution)/shard_map/ppermute | solution.py:19
  5.8 1.4 convert_reduce_fusion
  7.2 0.6 broadcast_in_dim.133
  7.9 5.5 %all-to-all-start = ((f32[8,1,1024]{2,1,0:T(1,128)}), f32[8,1,1024]{2,1,0:T(1,128)S(1)}, u32[]{:S(2)}, u32[]{:S(2)}) async-start(f32[8,1,1024]{2,1,0:T(1,128)} %broadcast_in_dim.133), calls=%async_computation | async-start | bytes 65536 | tf_op jit(solution)/shard_map/all_to_all | solution.py:14
  13.4 0.8 dynamic-slice_bitcast_fusion.2
  14.2 3.2 %collective-permute-start = (bf16[512,256]{1,0:T(8,128)(2,1)}, bf16[512,256]{1,0:T(8,128)(2,1)S(1)}, u32[]{:S(2)}, u32[]{:S(2)}) collective-permute-start(bf16[512,256]{1,0:T(8,128)(2,1)} %get-tuple-element.64), channel_id=1, source_target_pairs={{0,6},{2,0},{4,2},{6,4},{1,7},{3,1},{5,3},{7,5},{8,14},{10,8},{12,... | collective-permute-start | bytes 786440 | tf_op jit(solution)/shard_map/ppermute | solution.py:19
  17.5 0.9 collective-permute-start.1
  18.3 0.9 collective-permute-start.2
  19.2 8.9 %all-to-all-done = f32[8,1,1024]{2,1,0:T(1,128)S(1)} async-done(((f32[8,1,1024]{2,1,0:T(1,128)}), f32[8,1,1024]{2,1,0:T(1,128)S(1)}, u32[]{:S(2)}, u32[]{:S(2)}) %all-to-all-start) | async-done | bytes 32800 | tf_op jit(solution)/shard_map/all_to_all | solution.py:14
  28.2 0.7 collective-permute-done
  29.0 3.6 %collective-permute-start.8 = (bf16[256,1024]{1,0:T(8,128)(2,1)}, bf16[256,1024]{1,0:T(8,128)(2,1)S(1)}, u32[]{:S(2)}, u32[]{:S(2)}) collective-permute-start(bf16[256,1024]{1,0:T(8,128)(2,1)} %get-tuple-element.67), channel_id=1, source_target_pairs={{0,6},{2,0},{4,2},{6,4},{1,7},{3,1},{5,3},{7,5},{8,14},{10,8},{12,... | collective-permute-start | bytes 1572872 | tf_op jit(solution)/shard_map/ppermute | solution.py:19
  33.1 6.7 %collective-permute-start.3 = (bf16[2048,256]{1,0:T(8,128)(2,1)S(1)}, bf16[2048,256]{1,0:T(8,128)(2,1)S(1)}, u32[]{:S(2)}, u32[]{:S(2)}) collective-permute-start(bf16[2048,256]{1,0:T(8,128)(2,1)S(1)} %pad_maximum_fusion.2), channel_id=1, source_target_pairs={{0,112},{8,120},{16,0},{24,8},{32,16},{40,24},{48,32},{56,40},{64,... | collective-permute-start | bytes 3145736 | tf_op jit(solution)/shard_map/ppermute | solution.py:19
  39.9 2.6 %collective-permute-done.8 = bf16[256,1024]{1,0:T(8,128)(2,1)S(1)} collective-permute-done((bf16[256,1024]{1,0:T(8,128)(2,1)}, bf16[256,1024]{1,0:T(8,128)(2,1)S(1)}, u32[]{:S(2)}, u32[]{:S(2)}) %collective-permute-start.8) | collective-permute-done | bytes 524320 | tf_op jit(solution)/shard_map/ppermute | solution.py:19
  42.4 3.6 %collective-permute-start.11 = (bf16[256,1024]{1,0:T(8,128)(2,1)S(1)}, bf16[256,1024]{1,0:T(8,128)(2,1)S(1)}, u32[]{:S(2)}, u32[]{:S(2)}) collective-permute-start(bf16[256,1024]{1,0:T(8,128)(2,1)S(1)} %collective-permute-done.8), channel_id=1, source_target_pairs={{0,6},{2,0},{4,2},{6,4},{1,7},{3,1},{5,3},{7,5},{8,14},{10,8},{12,... | collective-permute-start | bytes 1572872 | tf_op jit(solution)/shard_map/ppermute | solution.py:19
  46.2 10.9 %collective-permute-done.10 = bf16[256,1024]{1,0:T(8,128)(2,1)S(1)} collective-permute-done((bf16[256,1024]{1,0:T(8,128)(2,1)S(1)}, bf16[256,1024]{1,0:T(8,128)(2,1)S(1)}, u32[]{:S(2)}, u32[]{:S(2)}) %collective-permute-start.10) | collective-permute-done | bytes 524320 | tf_op jit(solution)/shard_map/ppermute | solution.py:19
  57.7 1.3 convolution_convert_fusion.10
  59.0 0.6 copy-done.1
  59.6 1.3 collective-permute-start.13
  61.5 11.9 %collective-permute-done.13 = bf16[1024,256]{1,0:T(8,128)(2,1)S(1)} collective-permute-done((bf16[1024,256]{1,0:T(8,128)(2,1)S(1)}, bf16[1024,256]{1,0:T(8,128)(2,1)S(1)}, u32[]{:S(2)}, u32[]{:S(2)}) %collective-permute-start.13) | collective-permute-done | bytes 524320 | tf_op jit(solution)/shard_map/ppermute | solution.py:19
  74.3 3.8 %convolution_convert_fusion.9 = bf16[1024,256]{1,0:T(8,128)(2,1)S(1)} fusion(bf16[2048,1024]{1,0:T(8,128)(2,1)} %copy-done.1, bf16[2048,256]{1,0:T(8,128)(2,1)S(1)} %collective-permute-done.3), kind=kOutput, calls=%fused_computation.21 | convolution fusion | flops 1074003968 | bytes 5767168 | tf_op jit(solution)/shard_map/dot_general | solution.py:42
  78.1 0.9 collective-permute-start.19
  79.0 8.2 %collective-permute-done.5 = bf16[2048,256]{1,0:T(8,128)(2,1)S(1)} collective-permute-done((bf16[2048,256]{1,0:T(8,128)(2,1)S(1)}, bf16[2048,256]{1,0:T(8,128)(2,1)S(1)}, u32[]{:S(2)}, u32[]{:S(2)}) %collective-permute-start.5) | collective-permute-done | bytes 1048608 | tf_op jit(solution)/shard_map/ppermute | solution.py:19
  87.2 1.9 collective-permute-start.6
  89.4 1.3 convolution_convert_fusion
  90.8 3.6 %collective-permute-done.15 = f32[8,256]{1,0:T(8,128)S(1)} collective-permute-done((f32[8,256]{1,0:T(8,128)S(1)}, f32[8,256]{1,0:T(8,128)S(1)}, u32[]{:S(2)}, u32[]{:S(2)}) %collective-permute-start.15) | collective-permute-done | bytes 8224 | tf_op jit(solution)/shard_map/ppermute | solution.py:100
  94.8 6.1 %collective-permute-start.16 = (f32[8,256]{1,0:T(8,128)S(1)}, f32[8,256]{1,0:T(8,128)S(1)}, u32[]{:S(2)}, u32[]{:S(2)}) collective-permute-start(f32[8,256]{1,0:T(8,128)S(1)} %fusion.41), channel_id=1, source_target_pairs={{0,112},{8,120},{16,0},{24,8},{32,16},{40,24},{48,32},{56,40},{64,... | collective-permute-start | bytes 24584 | tf_op jit(solution)/shard_map/ppermute | solution.py:19
  101.0 0.8 collective-permute-done.18
  102.6 7.3 %collective-permute-done.6 = bf16[2048,256]{1,0:T(8,128)(2,1)S(1)} collective-permute-done((bf16[2048,256]{1,0:T(8,128)(2,1)S(1)}, bf16[2048,256]{1,0:T(8,128)(2,1)S(1)}, u32[]{:S(2)}, u32[]{:S(2)}) %collective-permute-start.6) | collective-permute-done | bytes 1048608 | tf_op jit(solution)/shard_map/ppermute | solution.py:24
  110.0 1.3 convolution_convert_fusion.7
  111.4 1.3 convolution_convert_fusion.8
  112.7 2.0 collective-permute-start.20
  115.0 9.6 %collective-permute-done.21 = bf16[1024,256]{1,0:T(8,128)(2,1)S(1)} collective-permute-done((bf16[1024,256]{1,0:T(8,128)(2,1)S(1)}, bf16[1024,256]{1,0:T(8,128)(2,1)S(1)}, u32[]{:S(2)}, u32[]{:S(2)}) %collective-permute-start.21) | collective-permute-done | bytes 524320 | tf_op jit(solution)/shard_map/ppermute | solution.py:19
  124.8 1.3 convolution_convert_fusion.1
  126.1 4.1 %collective-permute-done.20 = bf16[1024,256]{1,0:T(8,128)(2,1)S(1)} collective-permute-done((bf16[1024,256]{1,0:T(8,128)(2,1)S(1)}, bf16[1024,256]{1,0:T(8,128)(2,1)S(1)}, u32[]{:S(2)}, u32[]{:S(2)}) %collective-permute-start.20) | collective-permute-done | bytes 524320 | tf_op jit(solution)/shard_map/ppermute | solution.py:19
  130.5 1.3 convolution_convert_fusion.2
  133.2 4.1 %collective-permute-start.30 = (bf16[2048,256]{1,0:T(8,128)(2,1)S(1)}, bf16[2048,256]{1,0:T(8,128)(2,1)S(1)}, u32[]{:S(2)}, u32[]{:S(2)}) collective-permute-start(bf16[2048,256]{1,0:T(8,128)(2,1)S(1)} %convolution_convert_fusion.1), channel_id=1, source_target_pairs={{0,120},{8,0},{16,8},{24,16},{32,24},{40,32},{48,40},{56,48},{64,5... | collective-permute-start | bytes 3145736 | tf_op jit(solution)/shard_map/ppermute | solution.py:19
  137.9 0.6 collective-permute-start.35
  139.2 1.5 collective-permute-start.22
  140.7 1.8 collective-permute-start.25
  142.8 1.5 collective-permute-start.36
  144.3 1.3 fusion
  145.6 5.0 %collective-permute-done.25 = bf16[512,512]{1,0:T(8,128)(2,1)S(1)} collective-permute-done((bf16[512,512]{1,0:T(8,128)(2,1)S(1)}, bf16[512,512]{1,0:T(8,128)(2,1)S(1)}, u32[]{:S(2)}, u32[]{:S(2)}) %collective-permute-start.25) | collective-permute-done | bytes 524320 | tf_op jit(solution)/shard_map/ppermute | solution.py:19
  150.6 0.7 collective-permute-start.31
  151.4 0.6 fusion.2
  152.0 8.5 %collective-permute-done.36 = f32[8,256]{1,0:T(8,128)S(1)} collective-permute-done((f32[8,256]{1,0:T(8,128)S(1)}, f32[8,256]{1,0:T(8,128)S(1)}, u32[]{:S(2)}, u32[]{:S(2)}) %collective-permute-start.36) | collective-permute-done | bytes 8224 | tf_op jit(solution)/shard_map/ppermute | solution.py:100
  160.8 3.9 %collective-permute-start.26 = (bf16[512,512]{1,0:T(8,128)(2,1)S(1)}, bf16[512,512]{1,0:T(8,128)(2,1)S(1)}, u32[]{:S(2)}, u32[]{:S(2)}) collective-permute-start(bf16[512,512]{1,0:T(8,128)(2,1)S(1)} %fusion.2), channel_id=1, source_target_pairs={{0,6},{2,0},{4,2},{6,4},{1,7},{3,1},{5,3},{7,5},{8,14},{10,8},{12,... | collective-permute-start | bytes 1572872 | tf_op jit(solution)/shard_map/ppermute | solution.py:19
  164.7 0.6 fusion.1
  165.3 5.4 %collective-permute-start.38 = (f32[8,256]{1,0:T(8,128)S(1)}, f32[8,256]{1,0:T(8,128)S(1)}, u32[]{:S(2)}, u32[]{:S(2)}) collective-permute-start(f32[8,256]{1,0:T(8,128)S(1)} %select_select_fusion), channel_id=1, source_target_pairs={{0,104},{8,0},{16,120},{24,16},{32,8},{40,32},{48,24},{56,48},{64,... | collective-permute-start | bytes 24584 | tf_op jit(solution)/shard_map/ppermute | solution.py:34
  170.6 6.2 %collective-permute-done.29 = bf16[2048,256]{1,0:T(8,128)(2,1)S(1)} collective-permute-done((bf16[2048,256]{1,0:T(8,128)(2,1)S(1)}, bf16[2048,256]{1,0:T(8,128)(2,1)S(1)}, u32[]{:S(2)}, u32[]{:S(2)}) %collective-permute-start.29) | collective-permute-done | bytes 1048608 | tf_op jit(solution)/shard_map/ppermute | solution.py:19
  176.8 0.6 collective-permute-start.23
  178.1 10.5 %collective-permute-done.23 = bf16[512,512]{1,0:T(8,128)(2,1)S(1)} collective-permute-done((bf16[512,512]{1,0:T(8,128)(2,1)S(1)}, bf16[512,512]{1,0:T(8,128)(2,1)S(1)}, u32[]{:S(2)}, u32[]{:S(2)}) %collective-permute-start.23) | collective-permute-done | bytes 524320 | tf_op jit(solution)/shard_map/ppermute | solution.py:19
  188.6 1.7 collective-permute-start.40
  190.4 0.9 collective-permute-start.42
  191.2 2.4 %collective-permute-start.32 = (bf16[512,256]{1,0:T(8,128)(2,1)S(1)}, bf16[512,256]{1,0:T(8,128)(2,1)S(1)}, u32[]{:S(2)}, u32[]{:S(2)}) collective-permute-start(bf16[512,256]{1,0:T(8,128)(2,1)S(1)} %get-tuple-element.62), channel_id=1, source_target_pairs={{0,6},{2,0},{4,2},{6,4},{1,7},{3,1},{5,3},{7,5},{8,14},{10,8},{12,... | collective-permute-start | bytes 786440 | tf_op jit(solution)/shard_map/ppermute | solution.py:19
  193.7 2.2 %collective-permute-start.33 = (bf16[512,256]{1,0:T(8,128)(2,1)S(1)}, bf16[512,256]{1,0:T(8,128)(2,1)S(1)}, u32[]{:S(2)}, u32[]{:S(2)}) collective-permute-start(bf16[512,256]{1,0:T(8,128)(2,1)S(1)} %get-tuple-element.63), channel_id=1, source_target_pairs={{0,4},{2,6},{4,0},{6,2},{1,5},{3,7},{5,1},{7,3},{8,12},{10,14},{12... | collective-permute-start | bytes 786440 | tf_op jit(solution)/shard_map/ppermute | solution.py:19
  196.3 1.0 maximum_add_fusion
  197.3 0.7 collective-permute-done.40
  198.0 1.7 collective-permute-start.34
  200.2 0.9 collective-permute-done.41
  201.2 5.2 %collective-permute-done.42 = bf16[512,256]{1,0:T(8,128)(2,1)S(1)} collective-permute-done((bf16[512,256]{1,0:T(8,128)(2,1)S(1)}, bf16[512,256]{1,0:T(8,128)(2,1)S(1)}, u32[]{:S(2)}, u32[]{:S(2)}) %collective-permute-start.42) | collective-permute-done | bytes 262176 | tf_op jit(solution)/shard_map/ppermute | solution.py:19
  206.9 2.9 %collective-permute-done.33 = bf16[512,256]{1,0:T(8,128)(2,1)S(1)} collective-permute-done((bf16[512,256]{1,0:T(8,128)(2,1)S(1)}, bf16[512,256]{1,0:T(8,128)(2,1)S(1)}, u32[]{:S(2)}, u32[]{:S(2)}) %collective-permute-start.33) | collective-permute-done | bytes 262176 | tf_op jit(solution)/shard_map/ppermute | solution.py:19
  209.8 2.4 %collective-permute-done.34 = bf16[512,256]{1,0:T(8,128)(2,1)S(1)} collective-permute-done((bf16[512,256]{1,0:T(8,128)(2,1)S(1)}, bf16[512,256]{1,0:T(8,128)(2,1)S(1)}, u32[]{:S(2)}, u32[]{:S(2)}) %collective-permute-start.34) | collective-permute-done | bytes 262176 | tf_op jit(solution)/shard_map/ppermute | solution.py:19
  213.1 1.6 maximum_bitcast_fusion
  (98 shorter events, 11.5 us)
Async XLA Ops:
  0.6 12.8 %copy-start = (bf16[1,512,1024]{2,1,0:T(8,128)(2,1)S(1)}, bf16[1,512,1024]{2,1,0:T(8,128)(2,1)}, u32[]{:S(2)}) copy-start(bf16[1,512,1024]{2,1,0:T(8,128)(2,1)} %param.2) | copy-start | bytes 3145732
  3.0 43.0 %collective-permute-start.7 = (bf16[256,1024]{1,0:T(8,128)(2,1)}, bf16[256,1024]{1,0:T(8,128)(2,1)S(1)}, u32[]{:S(2)}, u32[]{:S(2)}) collective-permute-start(bf16[256,1024]{1,0:T(8,128)(2,1)} %get-tuple-element.68), channel_id=1, source_target_pairs={{0,6},{2,0},{4,2},{6,4},{1,7},{3,1},{5,3},{7,5},{8,14},{10,8},{12,... | collective-permute-start | bytes 1572872 | tf_op jit(solution)/shard_map/ppermute | solution.py:19
  5.8 27.1 %collective-permute-start.9 = (bf16[256,1024]{1,0:T(8,128)(2,1)}, bf16[256,1024]{1,0:T(8,128)(2,1)S(1)}, u32[]{:S(2)}, u32[]{:S(2)}) collective-permute-start(bf16[256,1024]{1,0:T(8,128)(2,1)} %get-tuple-element.68), channel_id=1, source_target_pairs={{0,2},{2,4},{4,6},{6,0},{1,3},{3,5},{5,7},{7,1},{8,10},{10,12},{12... | collective-permute-start | bytes 1572872 | tf_op jit(solution)/shard_map/ppermute | solution.py:19
  7.9 20.2 %all-to-all-start = ((f32[8,1,1024]{2,1,0:T(1,128)}), f32[8,1,1024]{2,1,0:T(1,128)S(1)}, u32[]{:S(2)}, u32[]{:S(2)}) async-start(f32[8,1,1024]{2,1,0:T(1,128)} %broadcast_in_dim.133), calls=%async_computation | async-start | bytes 65536 | tf_op jit(solution)/shard_map/all_to_all | solution.py:14
  14.2 14.7 %collective-permute-start = (bf16[512,256]{1,0:T(8,128)(2,1)}, bf16[512,256]{1,0:T(8,128)(2,1)S(1)}, u32[]{:S(2)}, u32[]{:S(2)}) collective-permute-start(bf16[512,256]{1,0:T(8,128)(2,1)} %get-tuple-element.64), channel_id=1, source_target_pairs={{0,6},{2,0},{4,2},{6,4},{1,7},{3,1},{5,3},{7,5},{8,14},{10,8},{12,... | collective-permute-start | bytes 786440 | tf_op jit(solution)/shard_map/ppermute | solution.py:19
  17.5 15.2 %collective-permute-start.1 = (bf16[512,256]{1,0:T(8,128)(2,1)S(1)}, bf16[512,256]{1,0:T(8,128)(2,1)S(1)}, u32[]{:S(2)}, u32[]{:S(2)}) collective-permute-start(bf16[512,256]{1,0:T(8,128)(2,1)S(1)} %get-tuple-element.66), channel_id=1, source_target_pairs={{0,4},{2,6},{4,0},{6,2},{1,5},{3,7},{5,1},{7,3},{8,12},{10,14},{12... | collective-permute-start | bytes 786440 | tf_op jit(solution)/shard_map/ppermute | solution.py:19
  18.3 14.4 %collective-permute-start.2 = (bf16[512,256]{1,0:T(8,128)(2,1)S(1)}, bf16[512,256]{1,0:T(8,128)(2,1)S(1)}, u32[]{:S(2)}, u32[]{:S(2)}) collective-permute-start(bf16[512,256]{1,0:T(8,128)(2,1)S(1)} %get-tuple-element.65), channel_id=1, source_target_pairs={{0,2},{2,4},{4,6},{6,0},{1,3},{3,5},{5,7},{7,1},{8,10},{10,12},{12... | collective-permute-start | bytes 786440 | tf_op jit(solution)/shard_map/ppermute | solution.py:19
  29.0 13.5 %collective-permute-start.8 = (bf16[256,1024]{1,0:T(8,128)(2,1)}, bf16[256,1024]{1,0:T(8,128)(2,1)S(1)}, u32[]{:S(2)}, u32[]{:S(2)}) collective-permute-start(bf16[256,1024]{1,0:T(8,128)(2,1)} %get-tuple-element.67), channel_id=1, source_target_pairs={{0,6},{2,0},{4,2},{6,4},{1,7},{3,1},{5,3},{7,5},{8,14},{10,8},{12,... | collective-permute-start | bytes 1572872 | tf_op jit(solution)/shard_map/ppermute | solution.py:19
  32.7 24.8 %collective-permute-start.12 = (bf16[256,1024]{1,0:T(8,128)(2,1)}, bf16[256,1024]{1,0:T(8,128)(2,1)S(1)}, u32[]{:S(2)}, u32[]{:S(2)}) collective-permute-start(bf16[256,1024]{1,0:T(8,128)(2,1)} %get-tuple-element.67), channel_id=1, source_target_pairs={{0,2},{2,4},{4,6},{6,0},{1,3},{3,5},{5,7},{7,1},{8,10},{10,12},{12... | collective-permute-start | bytes 1572872 | tf_op jit(solution)/shard_map/ppermute | solution.py:19
  33.0 24.2 %collective-permute-start.10 = (bf16[256,1024]{1,0:T(8,128)(2,1)S(1)}, bf16[256,1024]{1,0:T(8,128)(2,1)S(1)}, u32[]{:S(2)}, u32[]{:S(2)}) collective-permute-start(bf16[256,1024]{1,0:T(8,128)(2,1)S(1)} %collective-permute-done.9), channel_id=1, source_target_pairs={{0,2},{2,4},{4,6},{6,0},{1,3},{3,5},{5,7},{7,1},{8,10},{10,12},{12... | collective-permute-start | bytes 1572872 | tf_op jit(solution)/shard_map/ppermute | solution.py:19
  33.1 41.2 %collective-permute-start.3 = (bf16[2048,256]{1,0:T(8,128)(2,1)S(1)}, bf16[2048,256]{1,0:T(8,128)(2,1)S(1)}, u32[]{:S(2)}, u32[]{:S(2)}) collective-permute-start(bf16[2048,256]{1,0:T(8,128)(2,1)S(1)} %pad_maximum_fusion.2), channel_id=1, source_target_pairs={{0,112},{8,120},{16,0},{24,8},{32,16},{40,24},{48,32},{56,40},{64,... | collective-permute-start | bytes 3145736 | tf_op jit(solution)/shard_map/ppermute | solution.py:19
  42.4 14.9 %collective-permute-start.11 = (bf16[256,1024]{1,0:T(8,128)(2,1)S(1)}, bf16[256,1024]{1,0:T(8,128)(2,1)S(1)}, u32[]{:S(2)}, u32[]{:S(2)}) collective-permute-start(bf16[256,1024]{1,0:T(8,128)(2,1)S(1)} %collective-permute-done.8), channel_id=1, source_target_pairs={{0,6},{2,0},{4,2},{6,4},{1,7},{3,1},{5,3},{7,5},{8,14},{10,8},{12,... | collective-permute-start | bytes 1572872 | tf_op jit(solution)/shard_map/ppermute | solution.py:19
  57.6 2.0 copy-start.1
  57.6 3.3 %copy-start.3 = (f32[16,3]{0,1:T(4,128)S(1)}, f32[16,3]{0,1:T(4,128)}, u32[]{:S(2)}) copy-start(f32[16,3]{0,1:T(4,128)} %param.3) | copy-start | bytes 580
  59.6 13.8 %collective-permute-start.13 = (bf16[1024,256]{1,0:T(8,128)(2,1)S(1)}, bf16[1024,256]{1,0:T(8,128)(2,1)S(1)}, u32[]{:S(2)}, u32[]{:S(2)}) collective-permute-start(bf16[1024,256]{1,0:T(8,128)(2,1)S(1)} %convolution_convert_fusion.10), channel_id=1, source_target_pairs={{0,1},{1,0},{2,3},{3,2},{4,5},{5,4},{6,7},{7,6},{8,9},{9,8},{10,11... | collective-permute-start | bytes 1572872 | tf_op jit(solution)/shard_map/ppermute | solution.py:19
  61.5 25.7 %collective-permute-start.5 = (bf16[2048,256]{1,0:T(8,128)(2,1)S(1)}, bf16[2048,256]{1,0:T(8,128)(2,1)S(1)}, u32[]{:S(2)}, u32[]{:S(2)}) collective-permute-start(bf16[2048,256]{1,0:T(8,128)(2,1)S(1)} %pad_maximum_fusion.2), channel_id=1, source_target_pairs={{0,8},{8,16},{16,24},{24,32},{32,40},{40,48},{48,56},{56,64},{64,7... | collective-permute-start | bytes 3145736 | tf_op jit(solution)/shard_map/ppermute | solution.py:19
  73.8 15.7 %copy-start.2 = (bf16[2048,1024]{1,0:T(8,128)(2,1)S(1)}, bf16[2048,1024]{1,0:T(8,128)(2,1)}, u32[]{:S(2)}) copy-start(bf16[2048,1024]{1,0:T(8,128)(2,1)} %copy-done.1) | copy-start | bytes 12582916
  73.8 15.4 %collective-permute-start.14 = (f32[8,256]{1,0:T(8,128)S(1)}, f32[8,256]{1,0:T(8,128)S(1)}, u32[]{:S(2)}, u32[]{:S(2)}) collective-permute-start(f32[8,256]{1,0:T(8,128)S(1)} %broadcast_select_fusion.1), channel_id=1, source_target_pairs={{0,2},{2,0},{4,6},{6,4},{1,3},{3,1},{5,7},{7,5},{8,10},{10,8},{12,... | collective-permute-start | bytes 24584 | tf_op jit(solution)/shard_map/ppermute | solution.py:100
  78.1 24.2 %collective-permute-start.19 = (bf16[1024,256]{1,0:T(8,128)(2,1)S(1)}, bf16[1024,256]{1,0:T(8,128)(2,1)S(1)}, u32[]{:S(2)}, u32[]{:S(2)}) collective-permute-start(bf16[1024,256]{1,0:T(8,128)(2,1)S(1)} %convolution_convert_fusion.9), channel_id=1, source_target_pairs={{0,1},{1,0},{2,3},{3,2},{4,5},{5,4},{6,7},{7,6},{8,9},{9,8},{10,11... | collective-permute-start | bytes 1572872 | tf_op jit(solution)/shard_map/ppermute | solution.py:19
  87.2 22.6 %collective-permute-start.6 = (bf16[2048,256]{1,0:T(8,128)(2,1)S(1)}, bf16[2048,256]{1,0:T(8,128)(2,1)S(1)}, u32[]{:S(2)}, u32[]{:S(2)}) collective-permute-start(bf16[2048,256]{1,0:T(8,128)(2,1)S(1)} %collective-permute-done.5), channel_id=1, source_target_pairs={{0,16},{16,32},{32,48},{48,64},{64,80},{80,96},{96,112},{112,0},{1... | collective-permute-start | bytes 3145736 | tf_op jit(solution)/shard_map/ppermute | solution.py:24
  89.2 5.2 %collective-permute-start.15 = (f32[8,256]{1,0:T(8,128)S(1)}, f32[8,256]{1,0:T(8,128)S(1)}, u32[]{:S(2)}, u32[]{:S(2)}) collective-permute-start(f32[8,256]{1,0:T(8,128)S(1)} %fusion.45), channel_id=1, source_target_pairs={{0,4},{2,6},{4,0},{6,2},{1,5},{3,7},{5,1},{7,3},{8,12},{10,14},{12... | collective-permute-start | bytes 24584 | tf_op jit(solution)/shard_map/ppermute | solution.py:100
  94.5 7.2 %collective-permute-start.18 = (f32[8,256]{1,0:T(8,128)S(1)}, f32[8,256]{1,0:T(8,128)S(1)}, u32[]{:S(2)}, u32[]{:S(2)}) collective-permute-start(f32[8,256]{1,0:T(8,128)S(1)} %fusion.41), channel_id=1, source_target_pairs={{0,8},{8,32},{16,24},{24,48},{32,40},{40,64},{48,56},{56,80},{64,7... | collective-permute-start | bytes 24584 | tf_op jit(solution)/shard_map/ppermute | solution.py:34
  94.7 7.1 %collective-permute-start.17 = (f32[8,256]{1,0:T(8,128)S(1)}, f32[8,256]{1,0:T(8,128)S(1)}, u32[]{:S(2)}, u32[]{:S(2)}) collective-permute-start(f32[8,256]{1,0:T(8,128)S(1)} %fusion.41), channel_id=1, source_target_pairs={{0,120},{8,112},{16,8},{24,0},{32,24},{40,16},{48,40},{56,32},{64,... | collective-permute-start | bytes 24584 | tf_op jit(solution)/shard_map/ppermute | solution.py:34
  94.8 7.5 %collective-permute-start.16 = (f32[8,256]{1,0:T(8,128)S(1)}, f32[8,256]{1,0:T(8,128)S(1)}, u32[]{:S(2)}, u32[]{:S(2)}) collective-permute-start(f32[8,256]{1,0:T(8,128)S(1)} %fusion.41), channel_id=1, source_target_pairs={{0,112},{8,120},{16,0},{24,8},{32,16},{40,24},{48,32},{56,40},{64,... | collective-permute-start | bytes 24584 | tf_op jit(solution)/shard_map/ppermute | solution.py:19
  101.8 9.7 %collective-permute-start.4 = (bf16[2048,256]{1,0:T(8,128)(2,1)S(1)}, bf16[2048,256]{1,0:T(8,128)(2,1)S(1)}, u32[]{:S(2)}, u32[]{:S(2)}) collective-permute-start(bf16[2048,256]{1,0:T(8,128)(2,1)S(1)} %collective-permute-done.3), channel_id=1, source_target_pairs={{0,8},{8,0},{16,24},{24,16},{32,40},{40,32},{48,56},{56,48},{64,72... | collective-permute-start | bytes 3145736 | tf_op jit(solution)/shard_map/ppermute | solution.py:28
  111.3 13.3 %collective-permute-start.21 = (bf16[1024,256]{1,0:T(8,128)(2,1)S(1)}, bf16[1024,256]{1,0:T(8,128)(2,1)S(1)}, u32[]{:S(2)}, u32[]{:S(2)}) collective-permute-start(bf16[1024,256]{1,0:T(8,128)(2,1)S(1)} %convolution_convert_fusion.7), channel_id=1, source_target_pairs={{0,1},{1,0},{2,3},{3,2},{4,5},{5,4},{6,7},{7,6},{8,9},{9,8},{10,11... | collective-permute-start | bytes 1572872 | tf_op jit(solution)/shard_map/ppermute | solution.py:19
  112.7 17.5 %collective-permute-start.20 = (bf16[1024,256]{1,0:T(8,128)(2,1)S(1)}, bf16[1024,256]{1,0:T(8,128)(2,1)S(1)}, u32[]{:S(2)}, u32[]{:S(2)}) collective-permute-start(bf16[1024,256]{1,0:T(8,128)(2,1)S(1)} %convolution_convert_fusion.8), channel_id=1, source_target_pairs={{0,1},{1,0},{2,3},{3,2},{4,5},{5,4},{6,7},{7,6},{8,9},{9,8},{10,11... | collective-permute-start | bytes 1572872 | tf_op jit(solution)/shard_map/ppermute | solution.py:19
  131.8 11.0 %collective-permute-start.28 = (bf16[2048,256]{1,0:T(8,128)(2,1)S(1)}, bf16[2048,256]{1,0:T(8,128)(2,1)S(1)}, u32[]{:S(2)}, u32[]{:S(2)}) collective-permute-start(bf16[2048,256]{1,0:T(8,128)(2,1)S(1)} %convolution_convert_fusion.2), channel_id=1, source_target_pairs={{0,8},{8,0},{16,24},{24,16},{32,40},{40,32},{48,56},{56,48},{64,72... | collective-permute-start | bytes 3145736 | tf_op jit(solution)/shard_map/ppermute | solution.py:28
  133.2 17.4 %collective-permute-start.30 = (bf16[2048,256]{1,0:T(8,128)(2,1)S(1)}, bf16[2048,256]{1,0:T(8,128)(2,1)S(1)}, u32[]{:S(2)}, u32[]{:S(2)}) collective-permute-start(bf16[2048,256]{1,0:T(8,128)(2,1)S(1)} %convolution_convert_fusion.1), channel_id=1, source_target_pairs={{0,120},{8,0},{16,8},{24,16},{32,24},{40,32},{48,40},{56,48},{64,5... | collective-permute-start | bytes 3145736 | tf_op jit(solution)/shard_map/ppermute | solution.py:19
  137.9 4.6 %collective-permute-start.35 = (f32[8,256]{1,0:T(8,128)S(1)}, f32[8,256]{1,0:T(8,128)S(1)}, u32[]{:S(2)}, u32[]{:S(2)}) collective-permute-start(f32[8,256]{1,0:T(8,128)S(1)} %select_add_fusion), channel_id=1, source_target_pairs={{0,2},{2,0},{4,6},{6,4},{1,3},{3,1},{5,7},{7,5},{8,10},{10,8},{12,... | collective-permute-start | bytes 24584 | tf_op jit(solution)/shard_map/ppermute | solution.py:100
  139.2 21.6 %collective-permute-start.22 = (bf16[512,512]{1,0:T(8,128)(2,1)S(1)}, bf16[512,512]{1,0:T(8,128)(2,1)S(1)}, u32[]{:S(2)}, u32[]{:S(2)}) collective-permute-start(bf16[512,512]{1,0:T(8,128)(2,1)S(1)} %convolution_convert_fusion.6), channel_id=1, source_target_pairs={{0,2},{2,4},{4,6},{6,0},{1,3},{3,5},{5,7},{7,1},{8,10},{10,12},{12... | collective-permute-start | bytes 1572872 | tf_op jit(solution)/shard_map/ppermute | solution.py:19
  140.7 10.0 %collective-permute-start.25 = (bf16[512,512]{1,0:T(8,128)(2,1)S(1)}, bf16[512,512]{1,0:T(8,128)(2,1)S(1)}, u32[]{:S(2)}, u32[]{:S(2)}) collective-permute-start(bf16[512,512]{1,0:T(8,128)(2,1)S(1)} %convolution_convert_fusion.4), channel_id=1, source_target_pairs={{0,6},{2,0},{4,2},{6,4},{1,7},{3,1},{5,3},{7,5},{8,14},{10,8},{12,... | collective-permute-start | bytes 1572872 | tf_op jit(solution)/shard_map/ppermute | solution.py:19
  142.5 35.5 %collective-permute-start.27 = (bf16[512,512]{1,0:T(8,128)(2,1)S(1)}, bf16[512,512]{1,0:T(8,128)(2,1)S(1)}, u32[]{:S(2)}, u32[]{:S(2)}) collective-permute-start(bf16[512,512]{1,0:T(8,128)(2,1)S(1)} %convolution_convert_fusion.3), channel_id=1, source_target_pairs={{0,2},{2,4},{4,6},{6,0},{1,3},{3,5},{5,7},{7,1},{8,10},{10,12},{12... | collective-permute-start | bytes 1572872 | tf_op jit(solution)/shard_map/ppermute | solution.py:19
  142.8 17.7 %collective-permute-start.36 = (f32[8,256]{1,0:T(8,128)S(1)}, f32[8,256]{1,0:T(8,128)S(1)}, u32[]{:S(2)}, u32[]{:S(2)}) collective-permute-start(f32[8,256]{1,0:T(8,128)S(1)} %fusion.60), channel_id=1, source_target_pairs={{0,4},{2,6},{4,0},{6,2},{1,5},{3,7},{5,1},{7,3},{8,12},{10,14},{12... | collective-permute-start | bytes 24584 | tf_op jit(solution)/shard_map/ppermute | solution.py:100
  150.6 26.2 %collective-permute-start.29 = (bf16[2048,256]{1,0:T(8,128)(2,1)S(1)}, bf16[2048,256]{1,0:T(8,128)(2,1)S(1)}, u32[]{:S(2)}, u32[]{:S(2)}) collective-permute-start(bf16[2048,256]{1,0:T(8,128)(2,1)S(1)} %fusion), channel_id=1, source_target_pairs={{0,16},{8,24},{16,32},{24,40},{32,48},{40,56},{48,64},{56,72},{64,... | collective-permute-start | bytes 3145736 | tf_op jit(solution)/shard_map/ppermute | solution.py:19
  150.6 14.6 %collective-permute-start.31 = (bf16[2048,256]{1,0:T(8,128)(2,1)S(1)}, bf16[2048,256]{1,0:T(8,128)(2,1)S(1)}, u32[]{:S(2)}, u32[]{:S(2)}) collective-permute-start(bf16[2048,256]{1,0:T(8,128)(2,1)S(1)} %collective-permute-done.30), channel_id=1, source_target_pairs={{8,120},{24,8},{40,24},{56,40},{72,56},{88,72},{104,88},{120,104},... | collective-permute-start | bytes 3145736 | tf_op jit(solution)/shard_map/ppermute | solution.py:24
  160.5 17.4 %collective-permute-start.24 = (bf16[512,512]{1,0:T(8,128)(2,1)S(1)}, bf16[512,512]{1,0:T(8,128)(2,1)S(1)}, u32[]{:S(2)}, u32[]{:S(2)}) collective-permute-start(bf16[512,512]{1,0:T(8,128)(2,1)S(1)} %convolution_convert_fusion.5), channel_id=1, source_target_pairs={{0,6},{2,0},{4,2},{6,4},{1,7},{3,1},{5,3},{7,5},{8,14},{10,8},{12,... | collective-permute-start | bytes 1572872 | tf_op jit(solution)/shard_map/ppermute | solution.py:19
  160.8 29.6 %collective-permute-start.26 = (bf16[512,512]{1,0:T(8,128)(2,1)S(1)}, bf16[512,512]{1,0:T(8,128)(2,1)S(1)}, u32[]{:S(2)}, u32[]{:S(2)}) collective-permute-start(bf16[512,512]{1,0:T(8,128)(2,1)S(1)} %fusion.2), channel_id=1, source_target_pairs={{0,6},{2,0},{4,2},{6,4},{1,7},{3,1},{5,3},{7,5},{8,14},{10,8},{12,... | collective-permute-start | bytes 1572872 | tf_op jit(solution)/shard_map/ppermute | solution.py:19
  165.3 25.1 %collective-permute-start.38 = (f32[8,256]{1,0:T(8,128)S(1)}, f32[8,256]{1,0:T(8,128)S(1)}, u32[]{:S(2)}, u32[]{:S(2)}) collective-permute-start(f32[8,256]{1,0:T(8,128)S(1)} %select_select_fusion), channel_id=1, source_target_pairs={{0,104},{8,0},{16,120},{24,16},{32,8},{40,32},{48,24},{56,48},{64,... | collective-permute-start | bytes 24584 | tf_op jit(solution)/shard_map/ppermute | solution.py:34
  176.8 11.8 %collective-permute-start.23 = (bf16[512,512]{1,0:T(8,128)(2,1)S(1)}, bf16[512,512]{1,0:T(8,128)(2,1)S(1)}, u32[]{:S(2)}, u32[]{:S(2)}) collective-permute-start(bf16[512,512]{1,0:T(8,128)(2,1)S(1)} %fusion.1), channel_id=1, source_target_pairs={{0,2},{2,4},{4,6},{6,0},{1,3},{3,5},{5,7},{7,1},{8,10},{10,12},{12... | collective-permute-start | bytes 1572872 | tf_op jit(solution)/shard_map/ppermute | solution.py:19
  177.9 13.4 %collective-permute-start.39 = (f32[8,256]{1,0:T(8,128)S(1)}, f32[8,256]{1,0:T(8,128)S(1)}, u32[]{:S(2)}, u32[]{:S(2)}) collective-permute-start(f32[8,256]{1,0:T(8,128)S(1)} %select_select_fusion), channel_id=1, source_target_pairs={{0,24},{8,16},{16,40},{24,32},{32,56},{40,48},{48,72},{56,64},{64,... | collective-permute-start | bytes 24584 | tf_op jit(solution)/shard_map/ppermute | solution.py:34
  178.0 15.7 %collective-permute-start.37 = (f32[8,256]{1,0:T(8,128)S(1)}, f32[8,256]{1,0:T(8,128)S(1)}, u32[]{:S(2)}, u32[]{:S(2)}) collective-permute-start(f32[8,256]{1,0:T(8,128)S(1)} %select_select_fusion), channel_id=1, source_target_pairs={{0,16},{8,24},{16,32},{24,40},{32,48},{40,56},{48,64},{56,72},{64,... | collective-permute-start | bytes 24584 | tf_op jit(solution)/shard_map/ppermute | solution.py:19
  188.6 9.3 %collective-permute-start.40 = (bf16[512,256]{1,0:T(8,128)(2,1)S(1)}, bf16[512,256]{1,0:T(8,128)(2,1)S(1)}, u32[]{:S(2)}, u32[]{:S(2)}) collective-permute-start(bf16[512,256]{1,0:T(8,128)(2,1)S(1)} %get-tuple-element.60), channel_id=1, source_target_pairs={{0,6},{2,0},{4,2},{6,4},{1,7},{3,1},{5,3},{7,5},{8,14},{10,8},{12,... | collective-permute-start | bytes 786440 | tf_op jit(solution)/shard_map/ppermute | solution.py:19
  190.4 10.8 %collective-permute-start.41 = (bf16[512,256]{1,0:T(8,128)(2,1)S(1)}, bf16[512,256]{1,0:T(8,128)(2,1)S(1)}, u32[]{:S(2)}, u32[]{:S(2)}) collective-permute-start(bf16[512,256]{1,0:T(8,128)(2,1)S(1)} %get-tuple-element.59), channel_id=1, source_target_pairs={{0,4},{2,6},{4,0},{6,2},{1,5},{3,7},{5,1},{7,3},{8,12},{10,14},{12... | collective-permute-start | bytes 786440 | tf_op jit(solution)/shard_map/ppermute | solution.py:19
  190.4 15.9 %collective-permute-start.42 = (bf16[512,256]{1,0:T(8,128)(2,1)S(1)}, bf16[512,256]{1,0:T(8,128)(2,1)S(1)}, u32[]{:S(2)}, u32[]{:S(2)}) collective-permute-start(bf16[512,256]{1,0:T(8,128)(2,1)S(1)} %get-tuple-element.58), channel_id=1, source_target_pairs={{0,2},{2,4},{4,6},{6,0},{1,3},{3,5},{5,7},{7,1},{8,10},{10,12},{12... | collective-permute-start | bytes 786440 | tf_op jit(solution)/shard_map/ppermute | solution.py:19
  191.2 15.6 %collective-permute-start.32 = (bf16[512,256]{1,0:T(8,128)(2,1)S(1)}, bf16[512,256]{1,0:T(8,128)(2,1)S(1)}, u32[]{:S(2)}, u32[]{:S(2)}) collective-permute-start(bf16[512,256]{1,0:T(8,128)(2,1)S(1)} %get-tuple-element.62), channel_id=1, source_target_pairs={{0,6},{2,0},{4,2},{6,4},{1,7},{3,1},{5,3},{7,5},{8,14},{10,8},{12,... | collective-permute-start | bytes 786440 | tf_op jit(solution)/shard_map/ppermute | solution.py:19
  193.7 16.1 %collective-permute-start.33 = (bf16[512,256]{1,0:T(8,128)(2,1)S(1)}, bf16[512,256]{1,0:T(8,128)(2,1)S(1)}, u32[]{:S(2)}, u32[]{:S(2)}) collective-permute-start(bf16[512,256]{1,0:T(8,128)(2,1)S(1)} %get-tuple-element.63), channel_id=1, source_target_pairs={{0,4},{2,6},{4,0},{6,2},{1,5},{3,7},{5,1},{7,3},{8,12},{10,14},{12... | collective-permute-start | bytes 786440 | tf_op jit(solution)/shard_map/ppermute | solution.py:19
  198.0 14.2 %collective-permute-start.34 = (bf16[512,256]{1,0:T(8,128)(2,1)S(1)}, bf16[512,256]{1,0:T(8,128)(2,1)S(1)}, u32[]{:S(2)}, u32[]{:S(2)}) collective-permute-start(bf16[512,256]{1,0:T(8,128)(2,1)S(1)} %get-tuple-element.61), channel_id=1, source_target_pairs={{0,2},{2,4},{4,6},{6,0},{1,3},{3,5},{5,7},{7,1},{8,10},{10,12},{12... | collective-permute-start | bytes 786440 | tf_op jit(solution)/shard_map/ppermute | solution.py:19
